TPU v7x, 16 devices: a whole 2x2x2 slice. The times are simulated.
16 devices in a mesh: dp: 2 (over z), tp: 8 (over y, x, core).
Axes of the slice: x: 2, y: 2, z: 2, core: 2. Of those that a mesh axis runs over, the one named last changes fastest.
Arguments:
- tokens: int32 [64], P('dp'), parts along dimension 0
- positions: int32 [64], P('dp'), parts along dimension 0
- self_keys: bfloat16 [2, 64, 448, 16, 64], P(None, 'dp', None, 'tp'), parts along dimension 1
- self_vals: bfloat16 [2, 64, 448, 16, 64], P(None, 'dp', None, 'tp'), parts along dimension 1
- cross_keys: bfloat16 [2, 64, 1500, 16, 64], P(None, 'dp', None, 'tp'), parts along dimension 1
- cross_vals: bfloat16 [2, 64, 1500, 16, 64], P(None, 'dp', None, 'tp'), parts along dimension 1
- embed_table: bfloat16 [52224, 1024], P('tp')
- pos_table: bfloat16 [448, 1024], replicated
- w_qkv: bfloat16 [2, 1024, 3, 16, 64], P(None, None, None, 'tp')
- w_cq: bfloat16 [2, 1024, 16, 64], P(None, None, 'tp')
- in_bias: float32 [2, 3, 16, 64], P(None, None, 'tp')
- w_out: bfloat16 [2, 2, 16, 64, 1024], P(None, None, 'tp')
- out_bias: float32 [2, 3, 1024], replicated
- w_fc1: bfloat16 [2, 1024, 4096], P(None, None, 'tp')
- b_fc1: float32 [2, 4096], P(None, 'tp')
- w_fc2: bfloat16 [2, 4096, 1024], P(None, 'tp')
- ln_layers: float32 [2, 3, 2, 1024], replicated
- ln_final: float32 [2, 1024], replicated
Outputs:
- output 1: float32 [64, 52224], P('dp', 'tp'), parts along dimension 0
- output 2: bfloat16 [2, 64, 448, 16, 64], P(None, 'dp', None, 'tp'), parts along dimension 1
- output 3: bfloat16 [2, 64, 448, 16, 64], P(None, 'dp', None, 'tp'), parts along dimension 1
There are 2 independent parts. A program takes and returns all parts, laid end to end along the dimension named above; an argument that names none is the same for every part.
All inputs are finite; a program needn't handle non-finite values.
Results may differ from a plain program's by a relative error of at most 0.0122829.
Values are sent between devices in bfloat16 or wider.
A program may use at most 1 GiB of HBM per device.

v0:
```python
import jax
import jax.numpy as jnp
from jax import lax
from jax.sharding import PartitionSpec as P


def layer_norm(residual, ln_gain, ln_shift):
    row_mean = jnp.mean(residual, axis=-1, keepdims=True)
    centred = residual - row_mean
    variance = jnp.mean(centred * centred, axis=-1, keepdims=True)
    return (centred * lax.rsqrt(variance + 1e-5) * ln_gain + ln_shift).astype(jnp.bfloat16)


def cross_attend(queries, key_rows, val_rows):
    scores = jnp.einsum('bhe,bthe->bht', queries, key_rows, preferred_element_type=jnp.float32) * (queries.shape[-1] ** -0.5)
    weights = jax.nn.softmax(scores, axis=-1).astype(jnp.bfloat16)
    return jnp.einsum('bht,bthe->bhe', weights, val_rows, preferred_element_type=jnp.float32).astype(jnp.bfloat16)


def self_attend(queries, key_new, val_new, cache_keys, cache_vals, mask_add):
    qk_scale = queries.shape[-1] ** -0.5
    past_scores = jnp.einsum('bhe,bthe->bht', queries, cache_keys, preferred_element_type=jnp.float32) * qk_scale + mask_add
    new_score = jnp.einsum('bhe,bhe->bh', queries, key_new, preferred_element_type=jnp.float32)[:, :, None] * qk_scale
    score_peak = jnp.maximum(jnp.max(past_scores, axis=-1, keepdims=True), new_score)
    past_exp = jnp.exp(past_scores - score_peak)
    new_exp = jnp.exp(new_score - score_peak)
    denominator = jnp.sum(past_exp, axis=-1, keepdims=True) + new_exp
    past_weight = (past_exp / denominator).astype(jnp.bfloat16)
    new_weight = (new_exp / denominator).astype(jnp.bfloat16)
    mixed_vals = jnp.einsum('bht,bthe->bhe', past_weight, cache_vals, preferred_element_type=jnp.float32)
    mixed_vals = mixed_vals + new_weight.astype(jnp.float32) * val_new.astype(jnp.float32)
    return mixed_vals.astype(jnp.bfloat16)


def group_sum(part_sum):
    return lax.psum(part_sum, 'tp').astype(jnp.bfloat16).astype(jnp.float32)


def solution(mesh):
    def local_step(tokens, positions, self_keys, self_vals, cross_keys, cross_vals, embed_table, pos_table, w_qkv, w_cq, in_bias, w_out, out_bias, w_fc1, b_fc1, w_fc2, ln_layers, ln_final):
        shard_rows = embed_table.shape[0]
        local_ids = tokens - lax.axis_index('tp') * shard_rows
        owned_mask = (local_ids >= 0) & (local_ids < shard_rows)
        picked = jnp.take(embed_table, jnp.clip(local_ids, 0, shard_rows - 1), axis=0)
        picked = jnp.where(owned_mask[:, None], picked, jnp.zeros_like(picked))
        residual = lax.psum(picked, 'tp').astype(jnp.float32) + jnp.take(pos_table, positions, axis=0).astype(jnp.float32)
        cache_pos = jnp.arange(self_keys.shape[2])[None, :]
        mask_add = jnp.where(cache_pos < positions[:, None], 0.0, -1e30)[:, None, :]
        new_key_rows = []
        new_val_rows = []
        for layer_idx in range(self_keys.shape[0]):
            ln_params = ln_layers[layer_idx]
            bias_in = in_bias[layer_idx]
            hidden = layer_norm(residual, ln_params[0, 0], ln_params[0, 1])
            projected = jnp.einsum('bd,dthe->bthe', hidden, w_qkv[layer_idx], preferred_element_type=jnp.float32)
            queries = (projected[:, 0] + bias_in[0]).astype(jnp.bfloat16)
            key_new = projected[:, 1].astype(jnp.bfloat16)
            val_new = (projected[:, 2] + bias_in[1]).astype(jnp.bfloat16)
            attended = self_attend(queries, key_new, val_new, self_keys[layer_idx], self_vals[layer_idx], mask_add)
            head_sum = jnp.einsum('bhe,hed->bd', attended, w_out[layer_idx, 0], preferred_element_type=jnp.float32)
            residual = residual + group_sum(head_sum) + out_bias[layer_idx, 0]
            hidden = layer_norm(residual, ln_params[1, 0], ln_params[1, 1])
            cross_q = (jnp.einsum('bd,dhe->bhe', hidden, w_cq[layer_idx], preferred_element_type=jnp.float32) + bias_in[2]).astype(jnp.bfloat16)
            attended = cross_attend(cross_q, cross_keys[layer_idx], cross_vals[layer_idx])
            head_sum = jnp.einsum('bhe,hed->bd', attended, w_out[layer_idx, 1], preferred_element_type=jnp.float32)
            residual = residual + group_sum(head_sum) + out_bias[layer_idx, 1]
            hidden = layer_norm(residual, ln_params[2, 0], ln_params[2, 1])
            fc1_out = jnp.dot(hidden, w_fc1[layer_idx], preferred_element_type=jnp.float32) + b_fc1[layer_idx]
            active = jax.nn.gelu(fc1_out, approximate=False).astype(jnp.bfloat16)
            fc2_out = jnp.dot(active, w_fc2[layer_idx], preferred_element_type=jnp.float32)
            residual = residual + group_sum(fc2_out) + out_bias[layer_idx, 2]
            new_key_rows.append(key_new)
            new_val_rows.append(val_new)
        final_hidden = layer_norm(residual, ln_final[0], ln_final[1])
        logits = jnp.einsum('bd,vd->bv', final_hidden, embed_table, preferred_element_type=jnp.float32)
        write_mask = (cache_pos == positions[:, None])[None, :, :, None, None]
        new_keys = jnp.where(write_mask, jnp.stack(new_key_rows)[:, :, None], self_keys)
        new_vals = jnp.where(write_mask, jnp.stack(new_val_rows)[:, :, None], self_vals)
        return logits, new_keys, new_vals

    batch_spec = P('dp')
    cache_spec = P(None, 'dp', None, 'tp', None)
    in_specs = (batch_spec, batch_spec, cache_spec, cache_spec, cache_spec, cache_spec, P('tp', None), P(None, None), P(None, None, None, 'tp', None), P(None, None, 'tp', None), P(None, None, 'tp', None), P(None, None, 'tp', None, None), P(None, None, None), P(None, None, 'tp'), P(None, 'tp'), P(None, 'tp', None), P(None, None, None, None), P(None, None))
    out_specs = (P('dp', 'tp'), cache_spec, cache_spec)
    return jax.shard_map(local_step, mesh=mesh, in_specs=in_specs, out_specs=out_specs, check_vma=False)
```

profile of v0, /device:TPU:0, one launch (start us, length us, event | category | flops | bytes accessed | tf_op | source)
XLA Modules:
  0.0 288.3 jit_solution(10233641000177499617)
XLA Ops:
  7.3 0.8 compare_and_fusion.1
  8.1 7.2 %gather_fusion = bf16[32,1024]{1,0:T(8,128)(2,1)S(1)} fusion(bf16[6528,1024]{1,0:T(8,128)(2,1)} %param.24, s32[1024]{0:T(1024)S(1)} %pad_clamp_fusion.1), kind=kCustom, calls=%fused_computation | custom fusion | bytes 131200 | tf_op jit(solution)/shard_map/jit(_take)/gather | solution.py:44
  15.3 0.7 select_select_fusion
  16.0 0.7 compare_and_fusion
  16.7 0.7 compare_select_fusion
  17.3 0.7 iota_compare_fusion
  18.1 0.7 fusion.138
  18.8 0.8 fusion.321
  19.6 0.8 slice_bitcast_fusion.4
  20.3 0.8 fusion.320
  21.1 0.8 fusion.319
  21.9 0.8 slice_bitcast_fusion.2
  22.8 0.6 gather_fusion.1
  23.4 41.1 %all-reduce.8.cloned.1.call-done = bf16[32,1024]{1,0:T(8,128)(2,1)} async-done(((bf16[32,1024]{1,0:T(8,128)(2,1)}), bf16[32,1024]{1,0:T(8,128)(2,1)}) %all-reduce.8.cloned.1.call-update) | async-done | bytes 65552 | tf_op jit(solution)/shard_map/psum | solution.py:46
  64.5 1.1 fusion.80
  65.7 1.0 multiply_reduce_fusion.6
  66.7 1.7 fusion.50
  68.4 0.1 fusion.162
  68.5 2.8 fusion.22
  71.4 0.1 fusion.81
  71.5 0.2 fusion.78
  71.7 0.1 fusion.149
  71.8 3.4 %fusion.20 = f32[32,2,1,64]{3,2,1,0:T(1,128)S(1)} fusion(bf16[2,32,448,2,64]{2,4,3,1,0:T(8,128)(2,1)} %param.21, bf16[32,2,448,1]{2,0,1,3:T(8,128)(2,1)S(1)} %fusion.149), kind=kOutput, calls=%fused_computation.24 | convolution fusion | flops 3670016 | bytes 4268032 | tf_op jit(solution)/shard_map/bht,bthe->bhe/dot_general | solution.py:30
  75.2 0.3 convolution_bitcast_fusion.3
  75.5 23.5 %all-reduce.9 = bf16[32,1024]{1,0:T(8,128)(2,1)S(1)} all-reduce(f32[32,1024]{1,0:T(8,128)S(1)} %convolution_bitcast_fusion.3), channel_id=1, replica_groups=mesh['dp'=2,'tp'=8] {'tp'}, use_global_device_ids=true, to_apply=%region_5.6 | all-reduce | flops 32768 | bytes 196608 | tf_op jit(solution)/shard_map/psum | solution.py:36
  98.9 0.2 fusion.316
  99.2 0.2 multiply_reduce_fusion.5
  99.4 0.2 fusion.63
  99.7 6.3 %fusion.10 = f32[32,2,1,1500]{3,2,1,0:T(1,128)S(1)} fusion(bf16[2,32,1500,2,64]{2,4,3,1,0:T(8,128)(2,1)} %param.22, bf16[32,2,64,1]{2,1,0,3:T(2,128)(2,1)S(1)} %fusion.231), kind=kOutput, calls=%fused_computation.12 | convolution fusion | flops 12288000 | bytes 12975104 | tf_op jit(solution)/shard_map/bhe,bthe->bht/dot_general | solution.py:15
  106.0 0.3 fusion.36
  106.2 6.3 %fusion.8 = bf16[32,2,1,64]{3,2,1,0:T(2,128)(2,1)S(1)} fusion(bf16[2,32,1500,2,64]{2,4,3,1,0:T(8,128)(2,1)} %param.23, bf16[32,2,1500,1]{2,0,1,3:T(8,128)(2,1)S(1)} %fusion.36), kind=kOutput, calls=%fused_computation.10 | convolution fusion | flops 12288000 | bytes 12783104 | tf_op jit(solution)/shard_map/bht,bthe->bhe/dot_general | solution.py:17
  112.6 0.2 convolution_bitcast_fusion.2
  112.8 23.6 %all-reduce.10 = bf16[32,1024]{1,0:T(8,128)(2,1)S(1)} all-reduce(f32[32,1024]{1,0:T(8,128)S(1)} %convolution_bitcast_fusion.2), channel_id=1, replica_groups=mesh['dp'=2,'tp'=8] {'tp'}, use_global_device_ids=true, to_apply=%region_10.11 | all-reduce | flops 32768 | bytes 196608 | tf_op jit(solution)/shard_map/psum | solution.py:36
  136.4 0.1 fusion.315
  136.6 0.2 multiply_reduce_fusion.4
  136.8 2.3 fusion.41
  139.0 23.7 %all-reduce.11 = bf16[32,1024]{1,0:T(8,128)(2,1)S(1)} all-reduce(f32[32,1024]{1,0:T(8,128)S(1)} %fusion.41), channel_id=1, replica_groups=mesh['dp'=2,'tp'=8] {'tp'}, use_global_device_ids=true, to_apply=%region_13.14 | all-reduce | flops 32768 | bytes 196608 | tf_op jit(solution)/shard_map/psum | solution.py:36
  162.7 0.1 fusion.314
  162.8 0.2 multiply_reduce_fusion.3
  163.0 1.6 fusion.48
  164.8 0.1 fusion.159
  164.9 2.8 fusion.18
  167.7 0.1 fusion.82
  167.9 0.2 fusion.79
  168.1 0.1 fusion.150
  168.2 3.4 %fusion.16 = f32[32,2,1,64]{3,2,1,0:T(1,128)S(1)} fusion(bf16[2,32,448,2,64]{2,4,3,1,0:T(8,128)(2,1)} %param.21, bf16[32,2,448,1]{2,0,1,3:T(8,128)(2,1)S(1)} %fusion.150), kind=kOutput, calls=%fused_computation.20 | convolution fusion | flops 3670016 | bytes 4268032 | tf_op jit(solution)/shard_map/bht,bthe->bhe/dot_general | solution.py:30
  171.5 0.3 convolution_bitcast_fusion.1
  171.8 23.8 %all-reduce.12 = bf16[32,1024]{1,0:T(8,128)(2,1)S(1)} all-reduce(f32[32,1024]{1,0:T(8,128)S(1)} %convolution_bitcast_fusion.1), channel_id=1, replica_groups=mesh['dp'=2,'tp'=8] {'tp'}, use_global_device_ids=true, to_apply=%region_18.19 | all-reduce | flops 32768 | bytes 196608 | tf_op jit(solution)/shard_map/psum | solution.py:36
  195.7 0.1 fusion.313
  195.8 0.2 multiply_reduce_fusion.2
  196.0 0.3 fusion.59
  196.3 6.3 %fusion.6 = f32[32,2,1,1500]{3,2,1,0:T(1,128)S(1)} fusion(bf16[2,32,1500,2,64]{2,4,3,1,0:T(8,128)(2,1)} %param.22, bf16[32,2,64,1]{2,1,0,3:T(2,128)(2,1)S(1)} %fusion.232), kind=kOutput, calls=%fused_computation.8 | convolution fusion | flops 12288000 | bytes 12975104 | tf_op jit(solution)/shard_map/bhe,bthe->bht/dot_general | solution.py:15
  202.6 0.3 fusion.37
  202.9 6.3 %fusion.4 = bf16[32,2,1,64]{3,2,1,0:T(2,128)(2,1)S(1)} fusion(bf16[2,32,1500,2,64]{2,4,3,1,0:T(8,128)(2,1)} %param.23, bf16[32,2,1500,1]{2,0,1,3:T(8,128)(2,1)S(1)} %fusion.37), kind=kOutput, calls=%fused_computation.6 | convolution fusion | flops 12288000 | bytes 12783104 | tf_op jit(solution)/shard_map/bht,bthe->bhe/dot_general | solution.py:17
  209.2 0.2 convolution_bitcast_fusion
  209.5 23.6 %all-reduce.13 = bf16[32,1024]{1,0:T(8,128)(2,1)S(1)} all-reduce(f32[32,1024]{1,0:T(8,128)S(1)} %convolution_bitcast_fusion), channel_id=1, replica_groups=mesh['dp'=2,'tp'=8] {'tp'}, use_global_device_ids=true, to_apply=%region_23.24 | all-reduce | flops 32768 | bytes 196608 | tf_op jit(solution)/shard_map/psum | solution.py:36
  233.0 0.1 fusion.312
  233.2 0.2 multiply_reduce_fusion.1
  233.4 2.3 fusion.38
  235.7 23.6 %all-reduce.14 = bf16[32,1024]{1,0:T(8,128)(2,1)S(1)} all-reduce(f32[32,1024]{1,0:T(8,128)S(1)} %fusion.38), channel_id=1, replica_groups=mesh['dp'=2,'tp'=8] {'tp'}, use_global_device_ids=true, to_apply=%region_26.27 | all-reduce | flops 32768 | bytes 196608 | tf_op jit(solution)/shard_map/psum | solution.py:36
  259.2 0.1 fusion.311
  259.3 0.2 multiply_reduce_fusion
  259.5 9.7 %fusion.97 = f32[32,6528]{1,0:T(8,128)} fusion(bf16[6528,1024]{1,0:T(8,128)(2,1)} %param.24, f32[32,1024]{1,0:T(8,128)S(1)} %get-tuple-element.4, f32[1024]{0:T(1024)S(1)} %bitcast.258, f32[1024]{0:T(1024)S(1)} %bitcast.257, f32[32]{0:T(128)S(1)} %add_rsqrt_fusion, f32[32]{0:T(128)S(1)} %broadcast_multiply_fusion), kind=kOutput, calls=%fused_computation.134 | convolution fusion | flops 427982848 | bytes 14344448 | tf_op jit(solution)/shard_map/bd,vd->bv/dot_general | solution.py:75
  269.3 12.1 %broadcast_select_fusion = (bf16[2,32,448,2,64]{2,4,3,1,0:T(8,128)(2,1)}, bf16[2,32,448,2,64]{2,4,3,1,0:T(8,128)(2,1)}) fusion(bf16[2,32,448,2,64]{2,4,3,1,0:T(8,128)(2,1)} %param.21, pred[32,448]{1,0:T(8,128)(4,1)S(1)} %iota_compare_fusion, bf16[2,32,2,64]{3,2,1,0:T(2,128)(2,1)S(1)} %copy.28, bf16[2,32,448,2,64]{2,4,3,1,0:T(8,128)(2,1)} %param.20, ...), kind=kLoop, calls=%fused_computation.18 | loop fusion | flops 7340032 | bytes 29407232 | tf_op jit(solution)/shard_map/jit(_where)/select_n | solution.py:78
  (43 shorter events, 0.5 us)
Async XLA Ops:
  7.2 15.6 %copy-start = (bf16[448,1024]{1,0:T(8,128)(2,1)S(1)}, bf16[448,1024]{1,0:T(8,128)(2,1)}, u32[]{:S(2)}) copy-start(bf16[448,1024]{1,0:T(8,128)(2,1)} %param.25) | copy-start | bytes 2752516
  7.2 68.0 %copy-start.2 = (bf16[2,2,2,64,1024]{4,3,2,1,0:T(8,128)(2,1)S(1)}, bf16[2,2,2,64,1024]{4,3,2,1,0:T(8,128)(2,1)}, u32[]{:S(2)}) copy-start(bf16[2,2,2,64,1024]{4,3,2,1,0:T(8,128)(2,1)} %param.29) | copy-start | bytes 3145732
  7.2 92.2 %copy-start.4 = (bf16[2,1024,2,64]{1,3,2,0:T(8,128)(2,1)S(1)}, bf16[2,1024,2,64]{1,3,2,0:T(8,128)(2,1)}, u32[]{:S(2)}) copy-start(bf16[2,1024,2,64]{1,3,2,0:T(8,128)(2,1)} %param.27) | copy-start | bytes 1572868
  7.2 57.3 %all-reduce.8.cloned.1.call-start = ((), (), s32[]{:S(2)}) async-start(), calls=%async_computation | async-start | bytes 131072 | tf_op jit(solution)/shard_map/psum | solution.py:46
  64.5 34.4 %copy-start.3 = (bf16[32,1024]{1,0:T(8,128)(2,1)S(1)}, bf16[32,1024]{1,0:T(8,128)(2,1)}, u32[]{:S(2)}) copy-start(bf16[32,1024]{1,0:T(8,128)(2,1)} %all-reduce.8.cloned.1.call-done) | copy-start | bytes 196612
  269.3 12.1 %copy-start.1 = (bf16[448,1024]{1,0:T(8,128)(2,1)S(1)}, bf16[448,1024]{1,0:T(8,128)(2,1)}, u32[]{:S(2)}) copy-start(bf16[448,1024]{1,0:T(8,128)(2,1)} %param.25) | copy-start | bytes 2752516
Sparse Core Ops, SparseCore 0:
  16.1 48.3 all-reduce.7
where the time goes:
time: 289 us; the launch traced here: 288 us
  blocking collectives  142 us (49%)
  matrix products  56.8 us (20%)
  waiting for transfers between devices  41.2 us (14%)
  other arithmetic  22.4 us (8%)
  between operations  14.3 us (5%)
  local copies, waits for them, and re-layouts  11.8 us (4%)
    psum x6, blocking collectives, group_sum(): return lax.psum(part_sum, 'tp').astype(jnp.bfloat16).astype(jnp.float32)  142 us
    psum x1, waiting for transfers between devices, local_step(): lax.psum(picked, 'tp').astype(jnp.float32)  41.1 us
    dot_general x2, matrix products, cross_attend(): jnp.einsum('bht,bthe->bhe', weights, val_rows, preferred_element_type=jnp...  12.7 us
    dot_general x2, matrix products, cross_attend(): jnp.einsum('bhe,bthe->bht', queries, key_rows, preferred_element_type=jnp...  12.6 us
    select_n x1, other arithmetic, local_step(): jnp.where(write_mask, jnp.stack(new_val_rows)[:, :, None], self_vals)  12.1 us
    dot_general x1, matrix products, local_step(): jnp.einsum('bd,vd->bv', final_hidden, embed_table, preferred_element_type...  9.74 us
    gather x1, local copies, waits for them, and re-layouts, local_step(): jnp.take(embed_table, jnp.clip(local_ids, 0, shard_rows - 1), axis=0)  7.19 us
    dot_general x2, matrix products, self_attend(): jnp.einsum('bht,bthe->bhe', past_weight, cache_vals, preferred_element_ty...  6.73 us
  transfers between devices with their start and end apart: 1, of which 1 were waited for; matrix products, arithmetic and copies ran while one was open for 3% of the time, Pallas kernels for 0%

commit v1 on v0

v1 whole, which is shorter than its diff:
```python
import functools
import jax
import jax.numpy as jnp
from jax import lax
from jax.experimental import pallas as pl
from jax.experimental.pallas import tpu as pltpu
from jax.sharding import PartitionSpec as P

MESH = pl.DeviceIdType.MESH
F32 = jnp.float32
BF16 = jnp.bfloat16
NT = (((1,), (1,)), ((), ()))
TP = 8
HALVES = 2
PARITY = 2


def gather_kernel(tok_ref, pos_ref, emb_hbm, pos_hbm, picked_ref, posrow_ref, prow_ref, ebuf, pbuf, xbuf, ybuf, sem):
    shard_rows = emb_hbm.shape[0]
    n = tok_ref.shape[0]
    base = lax.axis_index('tp') * shard_rows

    def start(b, carry):
        tid = jnp.clip(tok_ref[b] - base, 0, shard_rows - 1)
        pid = pos_ref[b]
        pltpu.make_async_copy(emb_hbm.at[pl.ds(pl.multiple_of(tid // 8 * 8, 8), 8), :], ebuf.at[b], sem.at[0]).start()
        pltpu.make_async_copy(pos_hbm.at[pl.ds(pl.multiple_of(pid // 8 * 8, 8), 8), :], pbuf.at[b], sem.at[1]).start()
        return carry

    lax.fori_loop(0, n, start, 0)
    pltpu.make_async_copy(ebuf, ebuf, sem.at[0]).wait()
    pltpu.make_async_copy(pbuf, pbuf, sem.at[1]).wait()
    row8 = lax.broadcasted_iota(jnp.int32, (8, 1), 0)

    def pick(b, carry):
        tid = tok_ref[b] - base
        owned = (tid >= 0) & (tid < shard_rows)
        sub = jnp.where(owned, lax.rem(jnp.clip(tid, 0, shard_rows - 1), 8), 8)
        pid = pos_ref[b]
        erow = jnp.sum(jnp.where(row8 == sub, ebuf[b].astype(F32), 0.0), axis=0, keepdims=True)
        prow = jnp.sum(jnp.where(row8 == lax.rem(pid, 8), pbuf[b].astype(F32), 0.0), axis=0, keepdims=True)
        xbuf[pl.ds(b, 1), :] = erow
        ybuf[pl.ds(b, 1), :] = prow
        prow_ref[pl.ds(b, 1), :] = jnp.full((1, 128), pid, jnp.int32)
        return carry

    lax.fori_loop(0, n, pick, 0)
    picked_ref[...] = xbuf[...].astype(BF16)
    posrow_ref[...] = ybuf[...]


def norm_rows(x, ln):
    mean = jnp.mean(x, axis=-1, keepdims=True)
    centred = x - mean
    var = jnp.mean(centred * centred, axis=-1, keepdims=True)
    return (centred * lax.rsqrt(var + 1e-5) * ln[0:1, :] + ln[1:2, :]).astype(BF16)


def block_diag(q8):
    lane = lax.broadcasted_iota(jnp.int32, (8, 128), 1)
    qf = q8.astype(F32)
    both = jnp.concatenate([jnp.where(lane < 64, qf, 0.0), jnp.where(lane < 64, 0.0, qf)], axis=0)
    row = lax.rem(lax.broadcasted_iota(jnp.int32, (16, 128), 0), 8)
    blocks = [jnp.where(row == b, both, 0.0).astype(BF16) for b in range(8)]
    return both, jnp.concatenate(blocks, axis=1)


def fold_heads(o16):
    lane = lax.broadcasted_iota(jnp.int32, (8, 128), 1)
    row = lax.broadcasted_iota(jnp.int32, (8, 128), 0)
    out = jnp.zeros((8, 128), F32)
    for b in range(8):
        blk = jnp.where(lane < 64, o16[0:8, b * 128:(b + 1) * 128], o16[8:16, b * 128:(b + 1) * 128])
        out = jnp.where(row == b, blk, out)
    return out


def decoder_kernel(dims, pos_smem, picked_ref, posrow_ref, prow_ref, in_bias, out_bias, b_fc1, ln_layers, ln_final,
                   sk_hbm, sv_hbm, ck_hbm, cv_hbm, emb_hbm, wqkv_hbm, wcq_hbm, wout_hbm, fc1_hbm, fc2_hbm,
                   kvo, eo, fh_ref,
                   kbuf, vbuf, wqkv, wcq, wout, fc1, fc2,
                   xres, part, part0, rs_recv, rs_recv0, ag_full, qscr, oscr, knew, vnew,
                   self_sem, cross_sem, w_sem, e_sem, send_sem, recv_sem):
    layers, batch, ctx, frames = dims
    me = lax.axis_index('tp')
    ko, vo = kvo.at[0], kvo.at[1]
    hb = batch // HALVES
    rows_per = 128

    def self_copy(layer, which):
        src, dst = ((sk_hbm, ko), (sv_hbm, vo))[which]
        return pltpu.make_async_copy(src.at[layer], dst.at[layer], self_sem.at[layer, which])

    def cross_copy(layer, which, octet):
        src, dst = ((ck_hbm, kbuf), (cv_hbm, vbuf))[which]
        at = pl.ds(pl.multiple_of(octet * 1024, 1024), 1024)
        return pltpu.make_async_copy(src.at[layer, at, :], dst.at[at, :], cross_sem.at[layer, which, octet])

    weights = ((wqkv_hbm, wqkv), (wout_hbm, wout), (wcq_hbm, wcq), (fc1_hbm, fc1), (fc2_hbm, fc2))

    def w_copy(which, layer):
        src, dst = weights[which]
        return pltpu.make_async_copy(src.at[layer], dst.at[layer], w_sem.at[which, layer])

    w_copy(0, 0).start()
    self_copy(0, 0).start()
    self_copy(0, 1).start()
    w_copy(1, 0).start()
    w_copy(2, 0).start()
    for octet in range(batch // 8):
        cross_copy(0, 0, octet).start()
        cross_copy(0, 1, octet).start()
    w_copy(3, 0).start()
    w_copy(4, 0).start()
    w_copy(0, 1).start()
    self_copy(1, 0).start()
    self_copy(1, 1).start()
    for which in range(1, 5):
        w_copy(which, 1).start()

    barrier = pltpu.get_barrier_semaphore()
    for k in range(1, TP):
        pl.semaphore_signal(barrier, 1, device_id={'tp': lax.rem(me + k, TP)}, device_id_type=MESH)
    pl.semaphore_wait(barrier, TP - 1)

    def bufs(ph, s):
        if ph == 0:
            return part0.at[s], rs_recv0.at[s], ag_full.at[0, s]
        slot = ph % PARITY
        return part.at[slot, s], rs_recv.at[slot, s], ag_full.at[slot, s]

    def rs_start(ph, s):
        src, dst, _ = bufs(ph, s)
        for k in range(1, TP):
            peer = lax.rem(me + k, TP)
            pltpu.make_async_remote_copy(src.at[peer], dst.at[k - 1], send_sem.at[ph, s, 0], recv_sem.at[ph, s, 0],
                                         device_id={'tp': peer}, device_id_type=MESH).start()

    def wait_for(ref, sem):
        pltpu.make_async_copy(ref, ref, sem).wait()

    def rs_finish(ph, s):
        src, dst, full = bufs(ph, s)
        wait_for(dst, recv_sem.at[ph, s, 0])
        total = src[me].astype(F32)
        for k in range(TP - 1):
            total = total + dst[k].astype(F32)
        full[me] = total.astype(BF16)
        for k in range(1, TP):
            peer = lax.rem(me + k, TP)
            pltpu.make_async_remote_copy(full.at[me], full.at[me], send_sem.at[ph, s, 1], recv_sem.at[ph, s, 1],
                                         device_id={'tp': peer}, device_id_type=MESH).start()
        wait_for(dst, send_sem.at[ph, s, 0])

    def ag_finish(ph, s):
        _, _, full = bufs(ph, s)
        seven = full.at[pl.ds(0, TP - 1)]
        wait_for(seven, recv_sem.at[ph, s, 1])
        wait_for(seven, send_sem.at[ph, s, 1])
        return jnp.concatenate([full[j].astype(F32) for j in range(TP)], axis=1)

    def put_part(ph, s, value):
        dst = bufs(ph, s)[0]
        for j in range(TP):
            dst[j] = value[:, j * 128:(j + 1) * 128]

    def head_bias(layer, which):
        b = in_bias[layer, which]
        return jnp.concatenate([b[0:1, :], b[1:2, :]], axis=1)

    def half(s):
        return pl.ds(s * hb, hb)

    def self_block(layer, s):
        hidden = norm_rows(xres[half(s), :], ln_layers[layer, 0])
        proj = lax.dot_general(hidden, wqkv[layer], NT, preferred_element_type=F32)
        qscr[half(s), :] = (proj[:, 0:128] + head_bias(layer, 0)).astype(BF16).astype(F32)
        knew[layer, half(s), :] = proj[:, 128:256].astype(BF16).astype(F32)
        vnew[layer, half(s), :] = (proj[:, 256:384] + head_bias(layer, 1)).astype(BF16).astype(F32)

        def octet_body(i, carry):
            octet = s * (hb // 8) + i
            r8 = pl.ds(pl.multiple_of(octet * 8, 8), 8)
            at = pl.ds(pl.multiple_of(octet * 1024, 1024), 1024)
            both, qbd = block_diag(qscr[r8, :])
            p8 = prow_ref[r8, :][:, 0:1]
            past = jnp.dot(qbd, ko[layer, at, :], preferred_element_type=F32) * 0.125
            t = lax.broadcasted_iota(jnp.int32, (16, ctx), 1)
            past = jnp.where(t < jnp.concatenate([p8, p8], axis=0), past, -1e30)
            kn = knew[layer, r8, :]
            vn = vnew[layer, r8, :]
            new = jnp.sum(both * jnp.concatenate([kn, kn], axis=0), axis=1, keepdims=True) * 0.125
            peak = jnp.maximum(jnp.max(past, axis=1, keepdims=True), new)
            past_e = jnp.exp(past - peak)
            new_e = jnp.exp(new - peak)
            denom = jnp.sum(past_e, axis=1, keepdims=True) + new_e
            past_w = (past_e / denom).astype(BF16)
            new_w = (new_e / denom).astype(BF16).astype(F32)
            o16 = lax.dot_general(past_w, vo[layer, at, :], NT, preferred_element_type=F32)
            lane = lax.broadcasted_iota(jnp.int32, (8, 128), 1)
            oscr[r8, :] = fold_heads(o16) + jnp.where(lane < 64, new_w[0:8], new_w[8:16]) * vn
            return carry

        lax.fori_loop(0, hb // 8, octet_body, 0)
        return jnp.dot(oscr[half(s), :].astype(BF16), wout[layer, 0], preferred_element_type=F32)

    def cross_block(layer, s):
        hidden = norm_rows(xres[half(s), :], ln_layers[layer, 1])
        proj = lax.dot_general(hidden, wcq[layer], NT, preferred_element_type=F32)
        qscr[half(s), :] = (proj + head_bias(layer, 2)).astype(BF16).astype(F32)

        def octet_body(i, carry):
            octet = s * (hb // 8) + i
            r8 = pl.ds(pl.multiple_of(octet * 8, 8), 8)
            at = pl.ds(pl.multiple_of(octet * 1024, 1024), 1024)
            _, qbd = block_diag(qscr[r8, :])
            cross_copy(layer, 0, octet).wait()
            scores = jnp.dot(qbd, kbuf[at, :], preferred_element_type=F32) * 0.125
            if layer + 1 < layers:
                cross_copy(layer + 1, 0, octet).start()
            peak = jnp.max(scores, axis=1, keepdims=True)
            exps = jnp.exp(scores - peak)
            w = (exps / jnp.sum(exps, axis=1, keepdims=True)).astype(BF16)
            cross_copy(layer, 1, octet).wait()
            o16 = lax.dot_general(w, vbuf[at, :], NT, preferred_element_type=F32)
            if layer + 1 < layers:
                cross_copy(layer + 1, 1, octet).start()
            oscr[r8, :] = fold_heads(o16)
            return carry

        lax.fori_loop(0, hb // 8, octet_body, 0)
        return jnp.dot(oscr[half(s), :].astype(BF16), wout[layer, 1], preferred_element_type=F32)

    def mlp_block(layer, s):
        hidden = norm_rows(xres[half(s), :], ln_layers[layer, 2])
        pre = jnp.dot(hidden, fc1[layer], preferred_element_type=F32) + b_fc1[layer:layer + 1, :]
        active = (0.5 * pre * (1.0 + lax.erf(pre * (0.5 ** 0.5)))).astype(BF16)
        return jnp.dot(active, fc2[layer], preferred_element_type=F32)

    def write_new(layer, s):
        t = lax.broadcasted_iota(jnp.int32, (rows_per, ctx), 1)
        for new, cache in ((knew, ko), (vnew, vo)):
            cols = new[layer, half(s), :].T
            for i in range(hb):
                b = s * hb + i
                at = pl.ds(b * rows_per, rows_per)
                old = cache[layer, at, :].astype(F32)
                cache[layer, at, :] = jnp.where(t == pos_smem[b], cols[:, i:i + 1], old).astype(BF16)

    for s in range(HALVES):
        put_part(0, s, picked_ref[half(s), :])
        rs_start(0, s)
    for s in range(HALVES):
        rs_finish(0, s)
    for s in range(HALVES):
        xres[half(s), :] = ag_finish(0, s) + posrow_ref[half(s), :]
        if s == 0:
            w_copy(0, 0).wait()
            self_copy(0, 0).wait()
            self_copy(0, 1).wait()
            w_copy(1, 0).wait()
        put_part(1, s, self_block(0, s))
        rs_start(1, s)
    ph = 1
    for layer in range(layers):
        for kind in range(3):
            if kind == 0:
                for s in range(HALVES):
                    write_new(layer, s)
            if layer == 0 and kind == 0:
                pltpu.make_async_copy(emb_hbm, eo, e_sem).start()
            for s in range(HALVES):
                rs_finish(ph, s)
            for s in range(HALVES):
                xres[half(s), :] = xres[half(s), :] + ag_finish(ph, s) + out_bias[kind, layer:layer + 1, :]
                nxt = layer * 3 + kind + 1
                if nxt == layers * 3:
                    fh_ref[half(s), :] = norm_rows(xres[half(s), :], ln_final)
                    continue
                nl, nk = divmod(nxt, 3)
                if s == 0:
                    if nk == 0:
                        w_copy(0, nl).wait()
                        self_copy(nl, 0).wait()
                        self_copy(nl, 1).wait()
                        w_copy(1, nl).wait()
                    if nk == 1:
                        w_copy(2, nl).wait()
                    if nk == 2:
                        w_copy(3, nl).wait()
                        w_copy(4, nl).wait()
                put_part(ph + 1, s, (self_block, cross_block, mlp_block)[nk](nl, s))
                rs_start(ph + 1, s)
            ph += 1
    pltpu.make_async_copy(emb_hbm, eo, e_sem).wait()


def final_kernel(kv_ref, e_ref, fh_ref, logits_ref, ko_hbm, vo_hbm, sem):
    layers = kv_ref.shape[1]
    copies = []
    for layer in range(layers):
        for which, dst in enumerate((ko_hbm, vo_hbm)):
            c = pltpu.make_async_copy(kv_ref.at[which, layer], dst.at[layer], sem.at[layer, which])
            c.start()
            copies.append(c)
    fh = fh_ref[...]
    step = 384

    def body(i, carry):
        at = pl.ds(pl.multiple_of(i * step, step), step)
        logits_ref[:, at] = lax.dot_general(fh, e_ref[at, :], NT, preferred_element_type=F32)
        return carry

    lax.fori_loop(0, e_ref.shape[0] // step, body, 0)
    for c in copies:
        c.wait()


def solution(mesh):
    vm = pl.BlockSpec(memory_space=pltpu.VMEM)
    sm = pl.BlockSpec(memory_space=pltpu.SMEM)
    hbm = pl.BlockSpec(memory_space=pltpu.HBM)

    def local_step(tokens, positions, self_keys, self_vals, cross_keys, cross_vals, embed_table, pos_table, w_qkv, w_cq, in_bias, w_out, out_bias, w_fc1, b_fc1, w_fc2, ln_layers, ln_final):
        batch = tokens.shape[0]
        layers, _, ctx, heads, hd = self_keys.shape
        frames = cross_keys.shape[2]
        vocab, d = embed_table.shape
        ff = w_fc1.shape[2]
        rows = batch * heads * hd
        hb = batch // HALVES

        def flat(cache):
            return cache.transpose(0, 1, 3, 4, 2).reshape(layers, rows, cache.shape[2])

        picked, posrow, prow = pl.pallas_call(
            gather_kernel,
            out_shape=(jax.ShapeDtypeStruct((batch, d), BF16), jax.ShapeDtypeStruct((batch, d), F32), jax.ShapeDtypeStruct((batch, 128), jnp.int32)),
            in_specs=[sm, sm, hbm, hbm], out_specs=(vm, vm, vm),
            scratch_shapes=[pltpu.VMEM((batch, 8, d), BF16), pltpu.VMEM((batch, 8, d), BF16), pltpu.VMEM((batch, d), F32), pltpu.VMEM((batch, d), F32), pltpu.SemaphoreType.DMA((2,))],
            compiler_params=pltpu.CompilerParams(vmem_limit_bytes=60 * 2 ** 20),
            name='gather_rows',
        )(tokens, positions, embed_table, pos_table)

        kvo, eo, fh = pl.pallas_call(
            functools.partial(decoder_kernel, (layers, batch, ctx, frames)),
            out_shape=(pltpu.VMEM((2, layers, rows, ctx), BF16), pltpu.VMEM((vocab, d), BF16), jax.ShapeDtypeStruct((batch, d), BF16)),
            in_specs=[sm] + [vm] * 8 + [hbm] * 10,
            out_specs=(vm, vm, vm),
            scratch_shapes=[
                pltpu.VMEM((rows, frames), BF16), pltpu.VMEM((rows, frames), BF16),
                pltpu.VMEM((layers, 3 * heads * hd, d), BF16), pltpu.VMEM((layers, heads * hd, d), BF16),
                pltpu.VMEM((layers, 2, heads * hd, d), BF16), pltpu.VMEM((layers, d, ff), BF16), pltpu.VMEM((layers, ff, d), BF16),
                pltpu.VMEM((batch, d), F32),
                pltpu.VMEM((PARITY, HALVES, TP, hb, 128), F32), pltpu.VMEM((HALVES, TP, hb, 128), BF16),
                pltpu.VMEM((PARITY, HALVES, TP - 1, hb, 128), F32), pltpu.VMEM((HALVES, TP - 1, hb, 128), BF16),
                pltpu.VMEM((PARITY, HALVES, TP, hb, 128), BF16),
                pltpu.VMEM((batch, 128), F32), pltpu.VMEM((batch, 128), F32),
                pltpu.VMEM((layers, batch, 128), F32), pltpu.VMEM((layers, batch, 128), F32),
                pltpu.SemaphoreType.DMA((layers, 2)), pltpu.SemaphoreType.DMA((layers, 2, batch // 8)),
                pltpu.SemaphoreType.DMA((5, layers)), pltpu.SemaphoreType.DMA,
                pltpu.SemaphoreType.DMA((3 * layers + 1, HALVES, 2)), pltpu.SemaphoreType.DMA((3 * layers + 1, HALVES, 2)),
            ],
            compiler_params=pltpu.CompilerParams(collective_id=0, has_side_effects=True, vmem_limit_bytes=67 * 2 ** 19),
            name='decoder_layers',
        )(positions, picked, posrow, prow, in_bias, out_bias.transpose(1, 0, 2), b_fc1, ln_layers, ln_final,
          flat(self_keys), flat(self_vals), flat(cross_keys), flat(cross_vals), embed_table,
          w_qkv.transpose(0, 2, 3, 4, 1).reshape(layers, 3 * heads * hd, d), w_cq.transpose(0, 2, 3, 1).reshape(layers, heads * hd, d),
          w_out.reshape(layers, 2, heads * hd, d), w_fc1, w_fc2)

        logits, nk, nv = pl.pallas_call(
            final_kernel,
            out_shape=(jax.ShapeDtypeStruct((batch, vocab), F32), jax.ShapeDtypeStruct((layers, rows, ctx), BF16), jax.ShapeDtypeStruct((layers, rows, ctx), BF16)),
            in_specs=[vm] * 3, out_specs=(vm, hbm, hbm),
            scratch_shapes=[pltpu.SemaphoreType.DMA((layers, 2))],
            compiler_params=pltpu.CompilerParams(vmem_limit_bytes=2 * 2 ** 20),
            name='final_logits',
        )(kvo, eo, fh)

        def unflat(cache):
            return cache.reshape(layers, batch, heads, hd, ctx).transpose(0, 1, 4, 2, 3)

        return logits, unflat(nk), unflat(nv)

    batch_spec = P('dp')
    cache_spec = P(None, 'dp', None, 'tp', None)
    in_specs = (batch_spec, batch_spec, cache_spec, cache_spec, cache_spec, cache_spec, P('tp', None), P(None, None), P(None, None, None, 'tp', None), P(None, None, 'tp', None), P(None, None, 'tp', None), P(None, None, 'tp', None, None), P(None, None, None), P(None, None, 'tp'), P(None, 'tp'), P(None, 'tp', None), P(None, None, None, None), P(None, None))
    out_specs = (P('dp', 'tp'), cache_spec, cache_spec)
    return jax.shard_map(local_step, mesh=mesh, in_specs=in_specs, out_specs=out_specs, check_vma=False)
```

time: 289 us -> 85.7 us (0.30)
  blocking collectives: 142 us -> 0 us
  Pallas kernels: 0 us -> 83.8 us
  matrix products: 56.8 us -> 0 us
  waiting for transfers between devices: 41.2 us -> 0 us
  other arithmetic: 22.4 us -> 0 us
  between operations: 14.3 us -> 0.65 us
  local copies, waits for them, and re-layouts: 11.8 us -> 0.83 us
    psum x6 -> x0, blocking collectives: 142 us -> none  [group_sum(): return lax.psum(part_sum, 'tp').astype(jnp.bfloat16).astype(jnp.float32)]
    pallas_call x0 -> x3, Pallas kernels: none -> 83.8 us  [the longest x1 72.5 us: local_step(): pl.pallas_call(functools.partial(decoder_kernel, (layers, batch, ctx, fra...]
    dot_general x19 -> x0, matrix products: 56.8 us -> none  [the longest x2 12.7 us: cross_attend(): jnp.einsum('bht,bthe->bhe', weights, val_rows, preferred_element_type=jnp...]
    psum x1 -> x0, waiting for transfers between devices: 41.1 us -> none  [local_step(): lax.psum(picked, 'tp').astype(jnp.float32)]
    select_n x4 -> x0, other arithmetic: 14.2 us -> none  [the longest x1 12.1 us: local_step(): jnp.where(write_mask, jnp.stack(new_val_rows)[:, :, None], self_vals)]
    gather x2 -> x0, local copies, waits for them, and re-layouts: 7.82 us -> none  [the longest x1 7.19 us: local_step(): jnp.take(embed_table, jnp.clip(local_ids, 0, shard_rows - 1), axis=0)]
    reduce_sum x16 -> x0, other arithmetic: 4.54 us -> none  [the longest x7 2.2 us: layer_norm(): variance = jnp.mean(centred * centred, axis=-1, keepdims=True)]
  transfers between devices with their start and end apart: 1 -> 0, of which waited for: 1 -> 0; matrix products, arithmetic and copies ran while one was open for 3% -> 0% of each run, Pallas kernels for 0% -> 0%
where the time goes in v1:
time: 85.7 us; the launch traced here: 85.3 us
  Pallas kernels  83.8 us (98%)
    pallas_call x1, Pallas kernels, local_step(): pl.pallas_call(functools.partial(decoder_kernel, (layers, batch, ctx, fra...  72.5 us
    pallas_call x1, Pallas kernels, local_step(): pl.pallas_call(final_kernel, out_shape=(jax.ShapeDtypeStruct((batch, voca...  6.84 us
    pallas_call x1, Pallas kernels, local_step(): pl.pallas_call(gather_kernel, out_shape=(jax.ShapeDtypeStruct((batch, d),...  4.48 us

profile of v1, /device:TPU:0, one launch (start us, length us, event | category | flops | bytes accessed | tf_op | source)
XLA Modules:
  0.0 85.3 jit_solution(18303308962471855002)
XLA Ops:
  0.6 4.5 %gather_rows.1 = (bf16[32,1024]{1,0:T(8,128)(2,1)}, f32[32,1024]{1,0:T(8,128)}, s32[32,128]{1,0:T(8,128)}) custom-call(s32[32]{0:T(128)} %tok_ref.1, s32[32]{0:T(128)} %pos_smem.1, bf16[6528,1024]{1,0:T(8,128)(2,1)} %emb_hbm.3, bf16[448,1024]{1,0:T(8,128)(2,1)} %pos_hbm.1), custom_call_target="tpu_custom_call" | custom-call | tf_op jit(solution)/shard_map/gather_rows/pallas_call | solution.py:336
  5.1 72.5 %decoder_layers.1 = (bf16[2,2,4096,448]{3,2,1,0:T(8,128)(2,1)S(1)}, bf16[6528,1024]{1,0:T(8,128)(2,1)S(1)}, bf16[32,1024]{1,0:T(8,128)(2,1)}) custom-call(s32[32]{0:T(128)} %pos_smem.1, bf16[32,1024]{1,0:T(8,128)(2,1)} %get-tuple-element.12.picked_ref, f32[32,1024]{1,0:T(8,128)} %get-tuple-element.13.posrow_ref, s32[32,128]{1,0:T(8,128)} %get-tuple-element.14.prow_ref, ...), custom_call_target="tpu_custom_call" | custom-call | tf_op jit(solution)/shard_map/decoder_layers/pallas_call | solution.py:345
  77.6 0.0 copy-start
  77.6 0.8 copy-done
  78.4 6.8 %final_logits.1 = (f32[32,6528]{1,0:T(8,128)}, bf16[2,4096,448]{2,1,0:T(8,128)(2,1)}, bf16[2,4096,448]{2,1,0:T(8,128)(2,1)}) custom-call(bf16[2,2,4096,448]{3,2,1,0:T(8,128)(2,1)S(1)} %get-tuple-element.15.kv_ref, bf16[6528,1024]{1,0:T(8,128)(2,1)S(1)} %get-tuple-element.16.e_ref, bf16[32,1024]{1,0:T(8,128)(2,1)S(1)} %copy-done), custom_call_target="tpu_custom_call" | custom-call | tf_op jit(solution)/shard_map/final_logits/pallas_call | solution.py:371
Async XLA Ops:
  77.6 0.8 copy-start

commit v2 on v1

--- a/solution.py
+++ b/solution.py
@@ -10,12 +10,13 @@
 F32 = jnp.float32
 BF16 = jnp.bfloat16
 NT = (((1,), (1,)), ((), ()))
+TN = (((0,), (0,)), ((), ()))
 TP = 8
 HALVES = 2
 PARITY = 2
 
 
-def gather_kernel(tok_ref, pos_ref, emb_hbm, pos_hbm, picked_ref, posrow_ref, prow_ref, ebuf, pbuf, xbuf, ybuf, sem):
+def gather_kernel(tok_ref, pos_ref, tokv_ref, posv_ref, emb_hbm, pos_hbm, picked_ref, posrow_ref, ebuf, pbuf, sem):
     shard_rows = emb_hbm.shape[0]
     n = tok_ref.shape[0]
     base = lax.axis_index('tp') * shard_rows
@@ -23,30 +24,24 @@
     def start(b, carry):
         tid = jnp.clip(tok_ref[b] - base, 0, shard_rows - 1)
         pid = pos_ref[b]
-        pltpu.make_async_copy(emb_hbm.at[pl.ds(pl.multiple_of(tid // 8 * 8, 8), 8), :], ebuf.at[b], sem.at[0]).start()
-        pltpu.make_async_copy(pos_hbm.at[pl.ds(pl.multiple_of(pid // 8 * 8, 8), 8), :], pbuf.at[b], sem.at[1]).start()
+        at = pl.ds(pl.multiple_of(b * 16, 16), 16)
+        pltpu.make_async_copy(emb_hbm.at[pl.ds(pl.multiple_of(tid // 16 * 16, 16), 16), :], ebuf.at[at, :], sem.at[0]).start()
+        pltpu.make_async_copy(pos_hbm.at[pl.ds(pl.multiple_of(pid // 16 * 16, 16), 16), :], pbuf.at[at, :], sem.at[1]).start()
         return carry
 
-    lax.fori_loop(0, n, start, 0)
+    lax.fori_loop(0, n, start, 0, unroll=4)
+    tid = tokv_ref[...] - base
+    owned = (tid >= 0) & (tid < shard_rows)
+    lane16 = lax.broadcasted_iota(jnp.int32, (1, n), 1) * 16
+    tok_row = jnp.where(owned, lane16 + jnp.clip(tid, 0, shard_rows - 1) % 16, -1)
+    pos_row = lane16 + posv_ref[...] % 16
+    row = lax.broadcasted_iota(jnp.int32, (16 * n, n), 0)
+    tok_hot = jnp.where(row == tok_row, 1.0, 0.0).astype(BF16)
+    pos_hot = jnp.where(row == pos_row, 1.0, 0.0).astype(BF16)
     pltpu.make_async_copy(ebuf, ebuf, sem.at[0]).wait()
+    picked_ref[...] = lax.dot_general(tok_hot, ebuf[...], TN, preferred_element_type=F32).astype(BF16)
     pltpu.make_async_copy(pbuf, pbuf, sem.at[1]).wait()
-    row8 = lax.broadcasted_iota(jnp.int32, (8, 1), 0)
-
-    def pick(b, carry):
-        tid = tok_ref[b] - base
-        owned = (tid >= 0) & (tid < shard_rows)
-        sub = jnp.where(owned, lax.rem(jnp.clip(tid, 0, shard_rows - 1), 8), 8)
-        pid = pos_ref[b]
-        erow = jnp.sum(jnp.where(row8 == sub, ebuf[b].astype(F32), 0.0), axis=0, keepdims=True)
-        prow = jnp.sum(jnp.where(row8 == lax.rem(pid, 8), pbuf[b].astype(F32), 0.0), axis=0, keepdims=True)
-        xbuf[pl.ds(b, 1), :] = erow
-        ybuf[pl.ds(b, 1), :] = prow
-        prow_ref[pl.ds(b, 1), :] = jnp.full((1, 128), pid, jnp.int32)
-        return carry
-
-    lax.fori_loop(0, n, pick, 0)
-    picked_ref[...] = xbuf[...].astype(BF16)
-    posrow_ref[...] = ybuf[...]
+    posrow_ref[...] = lax.dot_general(pos_hot, pbuf[...], TN, preferred_element_type=F32)
 
 
 def norm_rows(x, ln):
@@ -75,12 +70,12 @@
     return out
 
 
-def decoder_kernel(dims, pos_smem, picked_ref, posrow_ref, prow_ref, in_bias, out_bias, b_fc1, ln_layers, ln_final,
+def decoder_kernel(dims, pos_smem, picked_ref, posrow_ref, in_bias_hbm, out_bias_hbm, b_fc1_hbm, ln_layers_hbm, ln_final_hbm,
                    sk_hbm, sv_hbm, ck_hbm, cv_hbm, emb_hbm, wqkv_hbm, wcq_hbm, wout_hbm, fc1_hbm, fc2_hbm,
                    kvo, eo, fh_ref,
-                   kbuf, vbuf, wqkv, wcq, wout, fc1, fc2,
+                   in_bias, out_bias, b_fc1, ln_layers, ln_final, kbuf, vbuf, wqkv, wcq, wout, fc1, fc2,
                    xres, part, part0, rs_recv, rs_recv0, ag_full, qscr, oscr, knew, vnew,
-                   self_sem, cross_sem, w_sem, e_sem, send_sem, recv_sem):
+                   small_sem, self_sem, cross_sem, w_sem, e_sem, send_sem, recv_sem):
     layers, batch, ctx, frames = dims
     me = lax.axis_index('tp')
     ko, vo = kvo.at[0], kvo.at[1]
@@ -102,21 +97,15 @@
         src, dst = weights[which]
         return pltpu.make_async_copy(src.at[layer], dst.at[layer], w_sem.at[which, layer])
 
+    small = [pltpu.make_async_copy(src, dst, small_sem.at[i]) for i, (src, dst) in enumerate((
+        (ln_layers_hbm, ln_layers), (in_bias_hbm, in_bias), (out_bias_hbm, out_bias), (b_fc1_hbm, b_fc1), (ln_final_hbm, ln_final)))]
+    for c in small:
+        c.start()
     w_copy(0, 0).start()
     self_copy(0, 0).start()
     self_copy(0, 1).start()
     w_copy(1, 0).start()
     w_copy(2, 0).start()
-    for octet in range(batch // 8):
-        cross_copy(0, 0, octet).start()
-        cross_copy(0, 1, octet).start()
-    w_copy(3, 0).start()
-    w_copy(4, 0).start()
-    w_copy(0, 1).start()
-    self_copy(1, 0).start()
-    self_copy(1, 1).start()
-    for which in range(1, 5):
-        w_copy(which, 1).start()
 
     barrier = pltpu.get_barrier_semaphore()
     for k in range(1, TP):
@@ -183,10 +172,13 @@
             r8 = pl.ds(pl.multiple_of(octet * 8, 8), 8)
             at = pl.ds(pl.multiple_of(octet * 1024, 1024), 1024)
             both, qbd = block_diag(qscr[r8, :])
-            p8 = prow_ref[r8, :][:, 0:1]
+            seq = lax.rem(lax.broadcasted_iota(jnp.int32, (16, 1), 0), 8)
+            limit = jnp.zeros((16, 1), jnp.int32)
+            for b in range(8):
+                limit = jnp.where(seq == b, pos_smem[octet * 8 + b], limit)
             past = jnp.dot(qbd, ko[layer, at, :], preferred_element_type=F32) * 0.125
             t = lax.broadcasted_iota(jnp.int32, (16, ctx), 1)
-            past = jnp.where(t < jnp.concatenate([p8, p8], axis=0), past, -1e30)
+            past = jnp.where(t < limit, past, -1e30)
             kn = knew[layer, r8, :]
             vn = vnew[layer, r8, :]
             new = jnp.sum(both * jnp.concatenate([kn, kn], axis=0), axis=1, keepdims=True) * 0.125
@@ -250,8 +242,13 @@
     for s in range(HALVES):
         put_part(0, s, picked_ref[half(s), :])
         rs_start(0, s)
+    for octet in range(batch // 8):
+        cross_copy(0, 0, octet).start()
+        cross_copy(0, 1, octet).start()
     for s in range(HALVES):
         rs_finish(0, s)
+    for c in small:
+        c.wait()
     for s in range(HALVES):
         xres[half(s), :] = ag_finish(0, s) + posrow_ref[half(s), :]
         if s == 0:
@@ -261,6 +258,8 @@
             w_copy(1, 0).wait()
         put_part(1, s, self_block(0, s))
         rs_start(1, s)
+    w_copy(3, 0).start()
+    w_copy(4, 0).start()
     ph = 1
     for layer in range(layers):
         for kind in range(3):
@@ -268,6 +267,12 @@
                 for s in range(HALVES):
                     write_new(layer, s)
             if layer == 0 and kind == 0:
+                w_copy(0, 1).start()
+                self_copy(1, 0).start()
+                self_copy(1, 1).start()
+                for which in range(1, 5):
+                    w_copy(which, 1).start()
+            if layer == 1 and kind == 0:
                 pltpu.make_async_copy(emb_hbm, eo, e_sem).start()
             for s in range(HALVES):
                 rs_finish(ph, s)
@@ -295,23 +300,32 @@
     pltpu.make_async_copy(emb_hbm, eo, e_sem).wait()
 
 
-def final_kernel(kv_ref, e_ref, fh_ref, logits_ref, ko_hbm, vo_hbm, sem):
-    layers = kv_ref.shape[1]
+def final_kernel(kv_ref, e_ref, fh_ref, logits_hbm, ko_hbm, vo_hbm, logits, sem, out_sem):
+    layers, rows = kv_ref.shape[1:3]
     copies = []
     for layer in range(layers):
         for which, dst in enumerate((ko_hbm, vo_hbm)):
-            c = pltpu.make_async_copy(kv_ref.at[which, layer], dst.at[layer], sem.at[layer, which])
-            c.start()
-            copies.append(c)
+            for part in range(4):
+                at = pl.ds(part * (rows // 4), rows // 4)
+                c = pltpu.make_async_copy(kv_ref.at[which, layer, at, :], dst.at[layer, at, :], sem.at[layer, which, part])
+                c.start()
+                copies.append(c)
     fh = fh_ref[...]
     step = 384
+    n = e_ref.shape[0] // step
+
+    def out_copy(i):
+        at = pl.ds(pl.multiple_of(i * step, step), step)
+        return pltpu.make_async_copy(logits.at[:, at], logits_hbm.at[:, at], out_sem)
 
     def body(i, carry):
         at = pl.ds(pl.multiple_of(i * step, step), step)
-        logits_ref[:, at] = lax.dot_general(fh, e_ref[at, :], NT, preferred_element_type=F32)
+        logits[:, at] = lax.dot_general(fh, e_ref[at, :], NT, preferred_element_type=F32)
+        out_copy(i).start()
         return carry
 
-    lax.fori_loop(0, e_ref.shape[0] // step, body, 0)
+    lax.fori_loop(0, n, body, 0)
+    pltpu.make_async_copy(logits, logits_hbm, out_sem).wait()
     for c in copies:
         c.wait()
 
@@ -333,21 +347,23 @@
         def flat(cache):
             return cache.transpose(0, 1, 3, 4, 2).reshape(layers, rows, cache.shape[2])
 
-        picked, posrow, prow = pl.pallas_call(
+        picked, posrow = pl.pallas_call(
             gather_kernel,
-            out_shape=(jax.ShapeDtypeStruct((batch, d), BF16), jax.ShapeDtypeStruct((batch, d), F32), jax.ShapeDtypeStruct((batch, 128), jnp.int32)),
-            in_specs=[sm, sm, hbm, hbm], out_specs=(vm, vm, vm),
-            scratch_shapes=[pltpu.VMEM((batch, 8, d), BF16), pltpu.VMEM((batch, 8, d), BF16), pltpu.VMEM((batch, d), F32), pltpu.VMEM((batch, d), F32), pltpu.SemaphoreType.DMA((2,))],
+            out_shape=(pltpu.VMEM((batch, d), BF16), pltpu.VMEM((batch, d), F32)),
+            in_specs=[sm, sm, vm, vm, hbm, hbm], out_specs=(vm, vm),
+            scratch_shapes=[pltpu.VMEM((16 * batch, d), BF16), pltpu.VMEM((16 * batch, d), BF16), pltpu.SemaphoreType.DMA((2,))],
             compiler_params=pltpu.CompilerParams(vmem_limit_bytes=60 * 2 ** 20),
             name='gather_rows',
-        )(tokens, positions, embed_table, pos_table)
-
+        )(tokens, positions, tokens.reshape(1, batch), positions.reshape(1, batch), embed_table, pos_table)
+
+        picked, posrow = (pltpu.with_memory_space_constraint(a, pltpu.VMEM) for a in (picked, posrow))
         kvo, eo, fh = pl.pallas_call(
             functools.partial(decoder_kernel, (layers, batch, ctx, frames)),
-            out_shape=(pltpu.VMEM((2, layers, rows, ctx), BF16), pltpu.VMEM((vocab, d), BF16), jax.ShapeDtypeStruct((batch, d), BF16)),
-            in_specs=[sm] + [vm] * 8 + [hbm] * 10,
+            out_shape=(pltpu.VMEM((2, layers, rows, ctx), BF16), pltpu.VMEM((vocab, d), BF16), pltpu.VMEM((batch, d), BF16)),
+            in_specs=[sm] + [vm] * 2 + [hbm] * 15,
             out_specs=(vm, vm, vm),
             scratch_shapes=[
+                pltpu.VMEM(in_bias.shape, F32), pltpu.VMEM((3, layers, d), F32), pltpu.VMEM(b_fc1.shape, F32), pltpu.VMEM(ln_layers.shape, F32), pltpu.VMEM(ln_final.shape, F32),
                 pltpu.VMEM((rows, frames), BF16), pltpu.VMEM((rows, frames), BF16),
                 pltpu.VMEM((layers, 3 * heads * hd, d), BF16), pltpu.VMEM((layers, heads * hd, d), BF16),
                 pltpu.VMEM((layers, 2, heads * hd, d), BF16), pltpu.VMEM((layers, d, ff), BF16), pltpu.VMEM((layers, ff, d), BF16),
@@ -357,13 +373,13 @@
                 pltpu.VMEM((PARITY, HALVES, TP, hb, 128), BF16),
                 pltpu.VMEM((batch, 128), F32), pltpu.VMEM((batch, 128), F32),
                 pltpu.VMEM((layers, batch, 128), F32), pltpu.VMEM((layers, batch, 128), F32),
-                pltpu.SemaphoreType.DMA((layers, 2)), pltpu.SemaphoreType.DMA((layers, 2, batch // 8)),
+                pltpu.SemaphoreType.DMA((5,)), pltpu.SemaphoreType.DMA((layers, 2)), pltpu.SemaphoreType.DMA((layers, 2, batch // 8)),
                 pltpu.SemaphoreType.DMA((5, layers)), pltpu.SemaphoreType.DMA,
                 pltpu.SemaphoreType.DMA((3 * layers + 1, HALVES, 2)), pltpu.SemaphoreType.DMA((3 * layers + 1, HALVES, 2)),
             ],
             compiler_params=pltpu.CompilerParams(collective_id=0, has_side_effects=True, vmem_limit_bytes=67 * 2 ** 19),
             name='decoder_layers',
-        )(positions, picked, posrow, prow, in_bias, out_bias.transpose(1, 0, 2), b_fc1, ln_layers, ln_final,
+        )(positions, picked, posrow, in_bias, out_bias.transpose(1, 0, 2), b_fc1, ln_layers, ln_final,
           flat(self_keys), flat(self_vals), flat(cross_keys), flat(cross_vals), embed_table,
           w_qkv.transpose(0, 2, 3, 4, 1).reshape(layers, 3 * heads * hd, d), w_cq.transpose(0, 2, 3, 1).reshape(layers, heads * hd, d),
           w_out.reshape(layers, 2, heads * hd, d), w_fc1, w_fc2)
@@ -371,8 +387,8 @@
         logits, nk, nv = pl.pallas_call(
             final_kernel,
             out_shape=(jax.ShapeDtypeStruct((batch, vocab), F32), jax.ShapeDtypeStruct((layers, rows, ctx), BF16), jax.ShapeDtypeStruct((layers, rows, ctx), BF16)),
-            in_specs=[vm] * 3, out_specs=(vm, hbm, hbm),
-            scratch_shapes=[pltpu.SemaphoreType.DMA((layers, 2))],
+            in_specs=[vm] * 3, out_specs=(hbm, hbm, hbm),
+            scratch_shapes=[pltpu.VMEM((batch, vocab), F32), pltpu.SemaphoreType.DMA((layers, 2, 4)), pltpu.SemaphoreType.DMA],
             compiler_params=pltpu.CompilerParams(vmem_limit_bytes=2 * 2 ** 20),
             name='final_logits',
         )(kvo, eo, fh)

time: 85.7 us -> 81.1 us (0.946)
  Pallas kernels: 83.8 us -> 80.1 us
    pallas_call x1, Pallas kernels: 72.5 us -> 69.8 us  [local_step(): pl.pallas_call(functools.partial(decoder_kernel, (layers, batch, ctx, fra...]
    pallas_call x1, Pallas kernels: 4.48 us -> 3.59 us  [local_step(): pl.pallas_call(gather_kernel, out_shape=(pltpu.VMEM((batch, d), BF16), pl...]
where the time goes in v2:
time: 81.1 us; the launch traced here: 80.8 us
  Pallas kernels  80.1 us (99%)
    pallas_call x1, Pallas kernels, local_step(): pl.pallas_call(functools.partial(decoder_kernel, (layers, batch, ctx, fra...  69.8 us
    pallas_call x1, Pallas kernels, local_step(): pl.pallas_call(final_kernel, out_shape=(jax.ShapeDtypeStruct((batch, voca...  6.69 us
    pallas_call x1, Pallas kernels, local_step(): pl.pallas_call(gather_kernel, out_shape=(pltpu.VMEM((batch, d), BF16), pl...  3.59 us

profile of v2, /device:TPU:0, one launch (start us, length us, event | category | flops | bytes accessed | tf_op | source)
XLA Modules:
  0.0 80.8 jit_solution(12839702725609504675)
XLA Ops:
  0.6 3.6 %gather_rows.1 = (bf16[32,1024]{1,0:T(8,128)(2,1)S(1)}, f32[32,1024]{1,0:T(8,128)S(1)}) custom-call(s32[32]{0:T(128)} %tok_ref.1, s32[32]{0:T(128)} %pos_smem.1, s32[1,32]{1,0:T(1,128)} %bitcast.37, s32[1,32]{1,0:T(1,128)} %bitcast.36, bf16[6528,1024]{1,0:T(8,128)(2,1)} %emb_hbm.3, bf16[448,1024]{1,0:T(8,128)(2,1)} %pos_hbm.1), custom_call_target="tpu_custom_call" | custom-call | tf_op jit(solution)/shard_map/gather_rows/pallas_call | solution.py:350
  4.2 69.8 %decoder_layers.1 = (bf16[2,2,4096,448]{3,2,1,0:T(8,128)(2,1)S(1)}, bf16[6528,1024]{1,0:T(8,128)(2,1)S(1)}, bf16[32,1024]{1,0:T(8,128)(2,1)S(1)}) custom-call(s32[32]{0:T(128)} %pos_smem.1, bf16[32,1024]{1,0:T(8,128)(2,1)S(1)} %get-tuple-element.11.picked_ref, f32[32,1024]{1,0:T(8,128)S(1)} %get-tuple-element.12.posrow_ref, f32[2,3,2,64]{3,2,1,0:T(2,128)} %in_bias_hbm.1, ...), custom_call_target="tpu_custom_call" | custom-call | tf_op jit(solution)/shard_map/decoder_layers/pallas_call | solution.py:360
  74.1 6.7 %final_logits.1 = (f32[32,6528]{1,0:T(8,128)}, bf16[2,4096,448]{2,1,0:T(8,128)(2,1)}, bf16[2,4096,448]{2,1,0:T(8,128)(2,1)}) custom-call(bf16[2,2,4096,448]{3,2,1,0:T(8,128)(2,1)S(1)} %get-tuple-element.13.kv_ref, bf16[6528,1024]{1,0:T(8,128)(2,1)S(1)} %get-tuple-element.14.e_ref, bf16[32,1024]{1,0:T(8,128)(2,1)S(1)} %get-tuple-element.15.fh_ref), custom_call_target="tpu_custom_call" | custom-call | tf_op jit(solution)/shard_map/final_logits/pallas_call | solution.py:387

commit v3 on v2

--- a/solution.py
+++ b/solution.py
@@ -101,6 +101,34 @@
         (ln_layers_hbm, ln_layers), (in_bias_hbm, in_bias), (out_bias_hbm, out_bias), (b_fc1_hbm, b_fc1), (ln_final_hbm, ln_final)))]
     for c in small:
         c.start()
+    e_rows = emb_hbm.shape[0] // 4
+
+    def e_copy(i):
+        at = pl.ds(i * e_rows, e_rows)
+        return pltpu.make_async_copy(emb_hbm.at[at, :], eo.at[at, :], e_sem.at[i])
+
+    pending = []
+
+    def pump(n):
+        for group in pending[:n]:
+            for c in group:
+                c.start()
+        del pending[:n]
+
+    for octet in range(batch // 8):
+        for which in range(2):
+            pending.append([cross_copy(0, which, octet)])
+    pending.append([w_copy(3, 0), w_copy(4, 0)])
+    pending.append([w_copy(0, 1), w_copy(1, 1), w_copy(2, 1)])
+    pending.append([self_copy(1, 0)])
+    pending.append([self_copy(1, 1)])
+    for octet in range(batch // 8):
+        for which in range(2):
+            pending.append([cross_copy(1, which, octet)])
+    pending.append([w_copy(3, 1), w_copy(4, 1)])
+    for i in range(4):
+        pending.append([e_copy(i)])
+
     w_copy(0, 0).start()
     self_copy(0, 0).start()
     self_copy(0, 1).start()
@@ -208,15 +236,11 @@
             _, qbd = block_diag(qscr[r8, :])
             cross_copy(layer, 0, octet).wait()
             scores = jnp.dot(qbd, kbuf[at, :], preferred_element_type=F32) * 0.125
-            if layer + 1 < layers:
-                cross_copy(layer + 1, 0, octet).start()
             peak = jnp.max(scores, axis=1, keepdims=True)
             exps = jnp.exp(scores - peak)
             w = (exps / jnp.sum(exps, axis=1, keepdims=True)).astype(BF16)
             cross_copy(layer, 1, octet).wait()
             o16 = lax.dot_general(w, vbuf[at, :], NT, preferred_element_type=F32)
-            if layer + 1 < layers:
-                cross_copy(layer + 1, 1, octet).start()
             oscr[r8, :] = fold_heads(o16)
             return carry
 
@@ -242,11 +266,10 @@
     for s in range(HALVES):
         put_part(0, s, picked_ref[half(s), :])
         rs_start(0, s)
-    for octet in range(batch // 8):
-        cross_copy(0, 0, octet).start()
-        cross_copy(0, 1, octet).start()
+    pump(2)
     for s in range(HALVES):
         rs_finish(0, s)
+    pump(2)
     for c in small:
         c.wait()
     for s in range(HALVES):
@@ -258,24 +281,16 @@
             w_copy(1, 0).wait()
         put_part(1, s, self_block(0, s))
         rs_start(1, s)
-    w_copy(3, 0).start()
-    w_copy(4, 0).start()
     ph = 1
     for layer in range(layers):
         for kind in range(3):
+            pump(2)
             if kind == 0:
                 for s in range(HALVES):
                     write_new(layer, s)
-            if layer == 0 and kind == 0:
-                w_copy(0, 1).start()
-                self_copy(1, 0).start()
-                self_copy(1, 1).start()
-                for which in range(1, 5):
-                    w_copy(which, 1).start()
-            if layer == 1 and kind == 0:
-                pltpu.make_async_copy(emb_hbm, eo, e_sem).start()
             for s in range(HALVES):
                 rs_finish(ph, s)
+            pump(2)
             for s in range(HALVES):
                 xres[half(s), :] = xres[half(s), :] + ag_finish(ph, s) + out_bias[kind, layer:layer + 1, :]
                 nxt = layer * 3 + kind + 1
@@ -297,7 +312,8 @@
                 put_part(ph + 1, s, (self_block, cross_block, mlp_block)[nk](nl, s))
                 rs_start(ph + 1, s)
             ph += 1
-    pltpu.make_async_copy(emb_hbm, eo, e_sem).wait()
+    for i in range(4):
+        e_copy(i).wait()
 
 
 def final_kernel(kv_ref, e_ref, fh_ref, logits_hbm, ko_hbm, vo_hbm, logits, sem, out_sem):
@@ -374,7 +390,7 @@
                 pltpu.VMEM((batch, 128), F32), pltpu.VMEM((batch, 128), F32),
                 pltpu.VMEM((layers, batch, 128), F32), pltpu.VMEM((layers, batch, 128), F32),
                 pltpu.SemaphoreType.DMA((5,)), pltpu.SemaphoreType.DMA((layers, 2)), pltpu.SemaphoreType.DMA((layers, 2, batch // 8)),
-                pltpu.SemaphoreType.DMA((5, layers)), pltpu.SemaphoreType.DMA,
+                pltpu.SemaphoreType.DMA((5, layers)), pltpu.SemaphoreType.DMA((4,)),
                 pltpu.SemaphoreType.DMA((3 * layers + 1, HALVES, 2)), pltpu.SemaphoreType.DMA((3 * layers + 1, HALVES, 2)),
             ],
             compiler_params=pltpu.CompilerParams(collective_id=0, has_side_effects=True, vmem_limit_bytes=67 * 2 ** 19),

time: 81.1 us -> 81 us (level)
  no operation moved by 1% of the time
where the time goes in v3:
time: 81 us; the launch traced here: 80.5 us
  Pallas kernels  79.8 us (99%)
    pallas_call x1, Pallas kernels, local_step(): pl.pallas_call(functools.partial(decoder_kernel, (layers, batch, ctx, fra...  69.7 us
    pallas_call x1, Pallas kernels, local_step(): pl.pallas_call(final_kernel, out_shape=(jax.ShapeDtypeStruct((batch, voca...  6.7 us
    pallas_call x1, Pallas kernels, local_step(): pl.pallas_call(gather_kernel, out_shape=(pltpu.VMEM((batch, d), BF16), pl...  3.49 us

profile of v3, /device:TPU:0, one launch (start us, length us, event | category | flops | bytes accessed | tf_op | source)
XLA Modules:
  0.0 80.5 jit_solution(50284603557015774)
XLA Ops:
  0.6 3.5 %gather_rows.1 = (bf16[32,1024]{1,0:T(8,128)(2,1)S(1)}, f32[32,1024]{1,0:T(8,128)S(1)}) custom-call(s32[32]{0:T(128)} %tok_ref.1, s32[32]{0:T(128)} %pos_smem.1, s32[1,32]{1,0:T(1,128)} %bitcast.37, s32[1,32]{1,0:T(1,128)} %bitcast.36, bf16[6528,1024]{1,0:T(8,128)(2,1)} %emb_hbm.3, bf16[448,1024]{1,0:T(8,128)(2,1)} %pos_hbm.1), custom_call_target="tpu_custom_call" | custom-call | tf_op jit(solution)/shard_map/gather_rows/pallas_call | solution.py:366
  4.1 69.7 %decoder_layers.1 = (bf16[2,2,4096,448]{3,2,1,0:T(8,128)(2,1)S(1)}, bf16[6528,1024]{1,0:T(8,128)(2,1)S(1)}, bf16[32,1024]{1,0:T(8,128)(2,1)S(1)}) custom-call(s32[32]{0:T(128)} %pos_smem.1, bf16[32,1024]{1,0:T(8,128)(2,1)S(1)} %get-tuple-element.11.picked_ref, f32[32,1024]{1,0:T(8,128)S(1)} %get-tuple-element.12.posrow_ref, f32[2,3,2,64]{3,2,1,0:T(2,128)} %in_bias_hbm.1, ...), custom_call_target="tpu_custom_call" | custom-call | tf_op jit(solution)/shard_map/decoder_layers/pallas_call | solution.py:376
  73.8 6.7 %final_logits.1 = (f32[32,6528]{1,0:T(8,128)}, bf16[2,4096,448]{2,1,0:T(8,128)(2,1)}, bf16[2,4096,448]{2,1,0:T(8,128)(2,1)}) custom-call(bf16[2,2,4096,448]{3,2,1,0:T(8,128)(2,1)S(1)} %get-tuple-element.13.kv_ref, bf16[6528,1024]{1,0:T(8,128)(2,1)S(1)} %get-tuple-element.14.e_ref, bf16[32,1024]{1,0:T(8,128)(2,1)S(1)} %get-tuple-element.15.fh_ref), custom_call_target="tpu_custom_call" | custom-call | tf_op jit(solution)/shard_map/final_logits/pallas_call | solution.py:403

commit v4 on v3

--- a/solution.py
+++ b/solution.py
@@ -12,7 +12,7 @@
 NT = (((1,), (1,)), ((), ()))
 TN = (((0,), (0,)), ((), ()))
 TP = 8
-HALVES = 2
+HALVES = 1
 PARITY = 2
 
 

time: 81 us -> 86.7 us (1.070)
  Pallas kernels: 79.8 us -> 85.7 us
    pallas_call x1, Pallas kernels: 69.7 us -> 75.5 us  [local_step(): pl.pallas_call(functools.partial(decoder_kernel, (layers, batch, ctx, fra...]
where the time goes in v4:
time: 86.7 us; the launch traced here: 86.3 us
  Pallas kernels  85.7 us (99%)
    pallas_call x1, Pallas kernels, local_step(): pl.pallas_call(functools.partial(decoder_kernel, (layers, batch, ctx, fra...  75.5 us
    pallas_call x1, Pallas kernels, local_step(): pl.pallas_call(final_kernel, out_shape=(jax.ShapeDtypeStruct((batch, voca...  6.69 us
    pallas_call x1, Pallas kernels, local_step(): pl.pallas_call(gather_kernel, out_shape=(pltpu.VMEM((batch, d), BF16), pl...  3.52 us

profile of v4, /device:TPU:0, one launch (start us, length us, event | category | flops | bytes accessed | tf_op | source)
XLA Modules:
  0.0 86.3 jit_solution(4317940342240164799)
XLA Ops:
  0.6 3.5 %gather_rows.1 = (bf16[32,1024]{1,0:T(8,128)(2,1)S(1)}, f32[32,1024]{1,0:T(8,128)S(1)}) custom-call(s32[32]{0:T(128)} %tok_ref.1, s32[32]{0:T(128)} %pos_smem.1, s32[1,32]{1,0:T(1,128)} %bitcast.37, s32[1,32]{1,0:T(1,128)} %bitcast.36, bf16[6528,1024]{1,0:T(8,128)(2,1)} %emb_hbm.3, bf16[448,1024]{1,0:T(8,128)(2,1)} %pos_hbm.1), custom_call_target="tpu_custom_call" | custom-call | tf_op jit(solution)/shard_map/gather_rows/pallas_call | solution.py:366
  4.2 75.5 %decoder_layers.1 = (bf16[2,2,4096,448]{3,2,1,0:T(8,128)(2,1)S(1)}, bf16[6528,1024]{1,0:T(8,128)(2,1)S(1)}, bf16[32,1024]{1,0:T(8,128)(2,1)S(1)}) custom-call(s32[32]{0:T(128)} %pos_smem.1, bf16[32,1024]{1,0:T(8,128)(2,1)S(1)} %get-tuple-element.11.picked_ref, f32[32,1024]{1,0:T(8,128)S(1)} %get-tuple-element.12.posrow_ref, f32[2,3,2,64]{3,2,1,0:T(2,128)} %in_bias_hbm.1, ...), custom_call_target="tpu_custom_call" | custom-call | tf_op jit(solution)/shard_map/decoder_layers/pallas_call | solution.py:376
  79.7 6.7 %final_logits.1 = (f32[32,6528]{1,0:T(8,128)}, bf16[2,4096,448]{2,1,0:T(8,128)(2,1)}, bf16[2,4096,448]{2,1,0:T(8,128)(2,1)}) custom-call(bf16[2,2,4096,448]{3,2,1,0:T(8,128)(2,1)S(1)} %get-tuple-element.13.kv_ref, bf16[6528,1024]{1,0:T(8,128)(2,1)S(1)} %get-tuple-element.14.e_ref, bf16[32,1024]{1,0:T(8,128)(2,1)S(1)} %get-tuple-element.15.fh_ref), custom_call_target="tpu_custom_call" | custom-call | tf_op jit(solution)/shard_map/final_logits/pallas_call | solution.py:403

commit v5 on v3

--- a/solution.py
+++ b/solution.py
@@ -74,7 +74,7 @@
                    sk_hbm, sv_hbm, ck_hbm, cv_hbm, emb_hbm, wqkv_hbm, wcq_hbm, wout_hbm, fc1_hbm, fc2_hbm,
                    kvo, eo, fh_ref,
                    in_bias, out_bias, b_fc1, ln_layers, ln_final, kbuf, vbuf, wqkv, wcq, wout, fc1, fc2,
-                   xres, part, part0, rs_recv, rs_recv0, ag_full, qscr, oscr, knew, vnew,
+                   xres, stage, stage0, pair, pair0, chips, chips0, full, qscr, oscr, knew, vnew,
                    small_sem, self_sem, cross_sem, w_sem, e_sem, send_sem, recv_sem):
     layers, batch, ctx, frames = dims
     me = lax.axis_index('tp')
@@ -140,46 +140,53 @@
         pl.semaphore_signal(barrier, 1, device_id={'tp': lax.rem(me + k, TP)}, device_id_type=MESH)
     pl.semaphore_wait(barrier, TP - 1)
 
+    core = lax.rem(me, 2)
+    chip = me // 2
+    partner = {'tp': 2 * chip + 1 - core}
+    wide = posrow_ref.shape[1] // 2
+
     def bufs(ph, s):
         if ph == 0:
-            return part0.at[s], rs_recv0.at[s], ag_full.at[0, s]
+            return stage0.at[s], pair0.at[s], chips0.at[s], full.at[0, s]
         slot = ph % PARITY
-        return part.at[slot, s], rs_recv.at[slot, s], ag_full.at[slot, s]
-
-    def rs_start(ph, s):
-        src, dst, _ = bufs(ph, s)
-        for k in range(1, TP):
-            peer = lax.rem(me + k, TP)
-            pltpu.make_async_remote_copy(src.at[peer], dst.at[k - 1], send_sem.at[ph, s, 0], recv_sem.at[ph, s, 0],
-                                         device_id={'tp': peer}, device_id_type=MESH).start()
+        return stage.at[slot, s], pair.at[slot, s], chips.at[slot, s], full.at[slot, s]
+
+    def send(src, dst, ph, s, step, device):
+        pltpu.make_async_remote_copy(src, dst, send_sem.at[ph, s, step], recv_sem.at[ph, s, step], device_id=device, device_id_type=MESH).start()
 
     def wait_for(ref, sem):
         pltpu.make_async_copy(ref, ref, sem).wait()
 
-    def rs_finish(ph, s):
-        src, dst, full = bufs(ph, s)
-        wait_for(dst, recv_sem.at[ph, s, 0])
-        total = src[me].astype(F32)
-        for k in range(TP - 1):
-            total = total + dst[k].astype(F32)
-        full[me] = total.astype(BF16)
-        for k in range(1, TP):
-            peer = lax.rem(me + k, TP)
-            pltpu.make_async_remote_copy(full.at[me], full.at[me], send_sem.at[ph, s, 1], recv_sem.at[ph, s, 1],
-                                         device_id={'tp': peer}, device_id_type=MESH).start()
-        wait_for(dst, send_sem.at[ph, s, 0])
-
-    def ag_finish(ph, s):
-        _, _, full = bufs(ph, s)
-        seven = full.at[pl.ds(0, TP - 1)]
-        wait_for(seven, recv_sem.at[ph, s, 1])
-        wait_for(seven, send_sem.at[ph, s, 1])
-        return jnp.concatenate([full[j].astype(F32) for j in range(TP)], axis=1)
-
-    def put_part(ph, s, value):
-        dst = bufs(ph, s)[0]
-        for j in range(TP):
-            dst[j] = value[:, j * 128:(j + 1) * 128]
+    def sum_start(ph, s, value):
+        mine, got, _, _ = bufs(ph, s)
+        mine[0] = value[:, :wide]
+        mine[1] = value[:, wide:]
+        send(mine.at[1 - core], got, ph, s, 0, partner)
+
+    def sum_chips(ph, s):
+        mine, got, by_chip, _ = bufs(ph, s)
+        wait_for(got, recv_sem.at[ph, s, 0])
+        by_chip[chip] = mine[core] + got[...]
+        for k in range(1, TP // 2):
+            send(by_chip.at[chip], by_chip.at[chip], ph, s, 1, {'tp': 2 * lax.rem(chip + k, TP // 2) + core})
+        wait_for(got, send_sem.at[ph, s, 0])
+
+    def sum_share(ph, s):
+        _, _, by_chip, both = bufs(ph, s)
+        others = by_chip.at[pl.ds(0, TP // 2 - 1)]
+        wait_for(others, recv_sem.at[ph, s, 1])
+        total = by_chip[0].astype(F32)
+        for q in range(1, TP // 2):
+            total = total + by_chip[q].astype(F32)
+        both[core] = total.astype(BF16)
+        send(both.at[core], both.at[core], ph, s, 2, partner)
+        wait_for(others, send_sem.at[ph, s, 1])
+
+    def sum_finish(ph, s):
+        both = bufs(ph, s)[3]
+        wait_for(both.at[0], recv_sem.at[ph, s, 2])
+        wait_for(both.at[0], send_sem.at[ph, s, 2])
+        return jnp.concatenate([both[0].astype(F32), both[1].astype(F32)], axis=1)
 
     def head_bias(layer, which):
         b = in_bias[layer, which]
@@ -188,17 +195,18 @@
     def half(s):
         return pl.ds(s * hb, hb)
 
-    def self_block(layer, s):
+    def self_block(layer, s, after_proj, middle):
         hidden = norm_rows(xres[half(s), :], ln_layers[layer, 0])
         proj = lax.dot_general(hidden, wqkv[layer], NT, preferred_element_type=F32)
         qscr[half(s), :] = (proj[:, 0:128] + head_bias(layer, 0)).astype(BF16).astype(F32)
         knew[layer, half(s), :] = proj[:, 128:256].astype(BF16).astype(F32)
         vnew[layer, half(s), :] = (proj[:, 256:384] + head_bias(layer, 1)).astype(BF16).astype(F32)
 
-        def octet_body(i, carry):
+        after_proj()
+        for i in range(hb // 8):
             octet = s * (hb // 8) + i
-            r8 = pl.ds(pl.multiple_of(octet * 8, 8), 8)
-            at = pl.ds(pl.multiple_of(octet * 1024, 1024), 1024)
+            r8 = pl.ds(octet * 8, 8)
+            at = pl.ds(octet * 1024, 1024)
             both, qbd = block_diag(qscr[r8, :])
             seq = lax.rem(lax.broadcasted_iota(jnp.int32, (16, 1), 0), 8)
             limit = jnp.zeros((16, 1), jnp.int32)
@@ -219,39 +227,40 @@
             o16 = lax.dot_general(past_w, vo[layer, at, :], NT, preferred_element_type=F32)
             lane = lax.broadcasted_iota(jnp.int32, (8, 128), 1)
             oscr[r8, :] = fold_heads(o16) + jnp.where(lane < 64, new_w[0:8], new_w[8:16]) * vn
-            return carry
-
-        lax.fori_loop(0, hb // 8, octet_body, 0)
+            if i == 0:
+                middle()
         return jnp.dot(oscr[half(s), :].astype(BF16), wout[layer, 0], preferred_element_type=F32)
 
-    def cross_block(layer, s):
+    def cross_block(layer, s, after_proj, middle):
         hidden = norm_rows(xres[half(s), :], ln_layers[layer, 1])
         proj = lax.dot_general(hidden, wcq[layer], NT, preferred_element_type=F32)
         qscr[half(s), :] = (proj + head_bias(layer, 2)).astype(BF16).astype(F32)
 
-        def octet_body(i, carry):
+        after_proj()
+        for i in range(hb // 8):
             octet = s * (hb // 8) + i
-            r8 = pl.ds(pl.multiple_of(octet * 8, 8), 8)
-            at = pl.ds(pl.multiple_of(octet * 1024, 1024), 1024)
+            r8 = pl.ds(octet * 8, 8)
+            at = pl.ds(octet * 1024, 1024)
             _, qbd = block_diag(qscr[r8, :])
             cross_copy(layer, 0, octet).wait()
             scores = jnp.dot(qbd, kbuf[at, :], preferred_element_type=F32) * 0.125
             peak = jnp.max(scores, axis=1, keepdims=True)
             exps = jnp.exp(scores - peak)
             w = (exps / jnp.sum(exps, axis=1, keepdims=True)).astype(BF16)
+            if i == 0:
+                middle()
             cross_copy(layer, 1, octet).wait()
             o16 = lax.dot_general(w, vbuf[at, :], NT, preferred_element_type=F32)
             oscr[r8, :] = fold_heads(o16)
-            return carry
-
-        lax.fori_loop(0, hb // 8, octet_body, 0)
         return jnp.dot(oscr[half(s), :].astype(BF16), wout[layer, 1], preferred_element_type=F32)
 
-    def mlp_block(layer, s):
+    def mlp_block(layer, s, after_proj, middle):
         hidden = norm_rows(xres[half(s), :], ln_layers[layer, 2])
         pre = jnp.dot(hidden, fc1[layer], preferred_element_type=F32) + b_fc1[layer:layer + 1, :]
         active = (0.5 * pre * (1.0 + lax.erf(pre * (0.5 ** 0.5)))).astype(BF16)
-        return jnp.dot(active, fc2[layer], preferred_element_type=F32)
+        out = jnp.dot(active, fc2[layer], preferred_element_type=F32)
+        middle()
+        return out
 
     def write_new(layer, s):
         t = lax.broadcasted_iota(jnp.int32, (rows_per, ctx), 1)
@@ -263,55 +272,63 @@
                 old = cache[layer, at, :].astype(F32)
                 cache[layer, at, :] = jnp.where(t == pos_smem[b], cols[:, i:i + 1], old).astype(BF16)
 
-    for s in range(HALVES):
-        put_part(0, s, picked_ref[half(s), :])
-        rs_start(0, s)
-    pump(2)
-    for s in range(HALVES):
-        rs_finish(0, s)
+    def nothing():
+        pass
+
+    def ready(nl, nk):
+        if nk == 0:
+            w_copy(0, nl).wait()
+            self_copy(nl, 0).wait()
+            self_copy(nl, 1).wait()
+            w_copy(1, nl).wait()
+        if nk == 1:
+            w_copy(2, nl).wait()
+        if nk == 2:
+            w_copy(3, nl).wait()
+            w_copy(4, nl).wait()
+
+    for s in range(2):
+        sum_start(0, s, picked_ref[half(s), :])
+    for s in range(2):
+        sum_chips(0, s)
     pump(2)
     for c in small:
         c.wait()
-    for s in range(HALVES):
-        xres[half(s), :] = ag_finish(0, s) + posrow_ref[half(s), :]
-        if s == 0:
-            w_copy(0, 0).wait()
-            self_copy(0, 0).wait()
-            self_copy(0, 1).wait()
-            w_copy(1, 0).wait()
-        put_part(1, s, self_block(0, s))
-        rs_start(1, s)
-    ph = 1
-    for layer in range(layers):
-        for kind in range(3):
-            pump(2)
-            if kind == 0:
-                for s in range(HALVES):
-                    write_new(layer, s)
-            for s in range(HALVES):
-                rs_finish(ph, s)
-            pump(2)
-            for s in range(HALVES):
-                xres[half(s), :] = xres[half(s), :] + ag_finish(ph, s) + out_bias[kind, layer:layer + 1, :]
-                nxt = layer * 3 + kind + 1
-                if nxt == layers * 3:
-                    fh_ref[half(s), :] = norm_rows(xres[half(s), :], ln_final)
-                    continue
-                nl, nk = divmod(nxt, 3)
-                if s == 0:
-                    if nk == 0:
-                        w_copy(0, nl).wait()
-                        self_copy(nl, 0).wait()
-                        self_copy(nl, 1).wait()
-                        w_copy(1, nl).wait()
-                    if nk == 1:
-                        w_copy(2, nl).wait()
-                    if nk == 2:
-                        w_copy(3, nl).wait()
-                        w_copy(4, nl).wait()
-                put_part(ph + 1, s, (self_block, cross_block, mlp_block)[nk](nl, s))
-                rs_start(ph + 1, s)
-            ph += 1
+    sum_share(0, 0)
+    for ph in range(3 * layers + 1):
+        layer, kind = divmod(ph, 3)
+        before, prev_kind = divmod(ph - 1, 3)
+
+        def update(s):
+            total = sum_finish(ph, s)
+            if ph == 0:
+                xres[half(s), :] = total + posrow_ref[half(s), :]
+            else:
+                xres[half(s), :] = xres[half(s), :] + total + out_bias[prev_kind, before:before + 1, :]
+
+        if ph == 3 * layers:
+            sum_share(ph, 1)
+            for s in range(2):
+                update(s)
+                fh_ref[half(s), :] = norm_rows(xres[half(s), :], ln_final)
+            break
+        block = (self_block, cross_block, mlp_block)[kind]
+        update(0)
+        ready(layer, kind)
+        share = functools.partial(sum_share, ph, 1)
+        sum_start(ph + 1, 0, block(layer, 0, share if kind < 2 else nothing, nothing))
+        if kind == 2:
+            share()
+        pump(2)
+        update(1)
+        sum_start(ph + 1, 1, block(layer, 1, nothing, functools.partial(sum_chips, ph + 1, 0)))
+        if kind == 0:
+            write_new(layer, 0)
+        sum_chips(ph + 1, 1)
+        pump(2)
+        if kind == 0:
+            write_new(layer, 1)
+        sum_share(ph + 1, 0)
     for i in range(4):
         e_copy(i).wait()
 
@@ -384,16 +401,17 @@
                 pltpu.VMEM((layers, 3 * heads * hd, d), BF16), pltpu.VMEM((layers, heads * hd, d), BF16),
                 pltpu.VMEM((layers, 2, heads * hd, d), BF16), pltpu.VMEM((layers, d, ff), BF16), pltpu.VMEM((layers, ff, d), BF16),
                 pltpu.VMEM((batch, d), F32),
-                pltpu.VMEM((PARITY, HALVES, TP, hb, 128), F32), pltpu.VMEM((HALVES, TP, hb, 128), BF16),
-                pltpu.VMEM((PARITY, HALVES, TP - 1, hb, 128), F32), pltpu.VMEM((HALVES, TP - 1, hb, 128), BF16),
-                pltpu.VMEM((PARITY, HALVES, TP, hb, 128), BF16),
+                pltpu.VMEM((PARITY, HALVES, 2, hb, d // 2), F32), pltpu.VMEM((HALVES, 2, hb, d // 2), BF16),
+                pltpu.VMEM((PARITY, HALVES, hb, d // 2), F32), pltpu.VMEM((HALVES, hb, d // 2), BF16),
+                pltpu.VMEM((PARITY, HALVES, TP // 2, hb, d // 2), F32), pltpu.VMEM((HALVES, TP // 2, hb, d // 2), BF16),
+                pltpu.VMEM((PARITY, HALVES, 2, hb, d // 2), BF16),
                 pltpu.VMEM((batch, 128), F32), pltpu.VMEM((batch, 128), F32),
                 pltpu.VMEM((layers, batch, 128), F32), pltpu.VMEM((layers, batch, 128), F32),
                 pltpu.SemaphoreType.DMA((5,)), pltpu.SemaphoreType.DMA((layers, 2)), pltpu.SemaphoreType.DMA((layers, 2, batch // 8)),
                 pltpu.SemaphoreType.DMA((5, layers)), pltpu.SemaphoreType.DMA((4,)),
-                pltpu.SemaphoreType.DMA((3 * layers + 1, HALVES, 2)), pltpu.SemaphoreType.DMA((3 * layers + 1, HALVES, 2)),
+                pltpu.SemaphoreType.DMA((3 * layers + 1, HALVES, 3)), pltpu.SemaphoreType.DMA((3 * layers + 1, HALVES, 3)),
             ],
-            compiler_params=pltpu.CompilerParams(collective_id=0, has_side_effects=True, vmem_limit_bytes=67 * 2 ** 19),
+            compiler_params=pltpu.CompilerParams(collective_id=0, has_side_effects=True, vmem_limit_bytes=139 * 2 ** 18),
             name='decoder_layers',
         )(positions, picked, posrow, in_bias, out_bias.transpose(1, 0, 2), b_fc1, ln_layers, ln_final,
           flat(self_keys), flat(self_vals), flat(cross_keys), flat(cross_vals), embed_table,

time: 81 us -> 79.4 us (0.980)
  Pallas kernels: 79.8 us -> 78.2 us
    pallas_call x1, Pallas kernels: 69.7 us -> 67.9 us  [local_step(): pl.pallas_call(functools.partial(decoder_kernel, (layers, batch, ctx, fra...]
where the time goes in v5:
time: 79.4 us; the launch traced here: 79.1 us
  Pallas kernels  78.2 us (98%)
  between operations  0.81 us (1%)
    pallas_call x1, Pallas kernels, local_step(): pl.pallas_call(functools.partial(decoder_kernel, (layers, batch, ctx, fra...  67.9 us
    pallas_call x1, Pallas kernels, local_step(): pl.pallas_call(final_kernel, out_shape=(jax.ShapeDtypeStruct((batch, voca...  6.69 us
    pallas_call x1, Pallas kernels, local_step(): pl.pallas_call(gather_kernel, out_shape=(pltpu.VMEM((batch, d), BF16), pl...  3.7 us

profile of v5, /device:TPU:0, one launch (start us, length us, event | category | flops | bytes accessed | tf_op | source)
XLA Modules:
  0.0 79.1 jit_solution(5017738748505461730)
XLA Ops:
  0.6 3.7 %gather_rows.1 = (bf16[32,1024]{1,0:T(8,128)(2,1)S(1)}, f32[32,1024]{1,0:T(8,128)S(1)}) custom-call(s32[32]{0:T(128)} %tok_ref.1, s32[32]{0:T(128)} %pos_smem.1, s32[1,32]{1,0:T(1,128)} %bitcast.37, s32[1,32]{1,0:T(1,128)} %bitcast.36, bf16[6528,1024]{1,0:T(8,128)(2,1)} %emb_hbm.3, bf16[448,1024]{1,0:T(8,128)(2,1)} %pos_hbm.1), custom_call_target="tpu_custom_call" | custom-call | tf_op jit(solution)/shard_map/gather_rows/pallas_call | solution.py:383
  4.3 67.9 %decoder_layers.1 = (bf16[2,2,4096,448]{3,2,1,0:T(8,128)(2,1)S(1)}, bf16[6528,1024]{1,0:T(8,128)(2,1)S(1)}, bf16[32,1024]{1,0:T(8,128)(2,1)S(1)}) custom-call(s32[32]{0:T(128)} %pos_smem.1, bf16[32,1024]{1,0:T(8,128)(2,1)S(1)} %get-tuple-element.11.picked_ref, f32[32,1024]{1,0:T(8,128)S(1)} %get-tuple-element.12.posrow_ref, f32[2,3,2,64]{3,2,1,0:T(2,128)} %in_bias_hbm.1, ...), custom_call_target="tpu_custom_call" | custom-call | tf_op jit(solution)/shard_map/decoder_layers/pallas_call | solution.py:393
  72.2 6.7 %final_logits.1 = (f32[32,6528]{1,0:T(8,128)}, bf16[2,4096,448]{2,1,0:T(8,128)(2,1)}, bf16[2,4096,448]{2,1,0:T(8,128)(2,1)}) custom-call(bf16[2,2,4096,448]{3,2,1,0:T(8,128)(2,1)S(1)} %get-tuple-element.13.kv_ref, bf16[6528,1024]{1,0:T(8,128)(2,1)S(1)} %get-tuple-element.14.e_ref, bf16[32,1024]{1,0:T(8,128)(2,1)S(1)} %get-tuple-element.15.fh_ref), custom_call_target="tpu_custom_call" | custom-call | tf_op jit(solution)/shard_map/final_logits/pallas_call | solution.py:421

commit v6 on v5

--- a/solution.py
+++ b/solution.py
@@ -195,14 +195,13 @@
     def half(s):
         return pl.ds(s * hb, hb)
 
-    def self_block(layer, s, after_proj, middle):
+    def self_block(layer, s, early, late):
         hidden = norm_rows(xres[half(s), :], ln_layers[layer, 0])
         proj = lax.dot_general(hidden, wqkv[layer], NT, preferred_element_type=F32)
         qscr[half(s), :] = (proj[:, 0:128] + head_bias(layer, 0)).astype(BF16).astype(F32)
         knew[layer, half(s), :] = proj[:, 128:256].astype(BF16).astype(F32)
         vnew[layer, half(s), :] = (proj[:, 256:384] + head_bias(layer, 1)).astype(BF16).astype(F32)
 
-        after_proj()
         for i in range(hb // 8):
             octet = s * (hb // 8) + i
             r8 = pl.ds(octet * 8, 8)
@@ -227,16 +226,13 @@
             o16 = lax.dot_general(past_w, vo[layer, at, :], NT, preferred_element_type=F32)
             lane = lax.broadcasted_iota(jnp.int32, (8, 128), 1)
             oscr[r8, :] = fold_heads(o16) + jnp.where(lane < 64, new_w[0:8], new_w[8:16]) * vn
-            if i == 0:
-                middle()
         return jnp.dot(oscr[half(s), :].astype(BF16), wout[layer, 0], preferred_element_type=F32)
 
-    def cross_block(layer, s, after_proj, middle):
+    def cross_block(layer, s, early, late):
         hidden = norm_rows(xres[half(s), :], ln_layers[layer, 1])
         proj = lax.dot_general(hidden, wcq[layer], NT, preferred_element_type=F32)
         qscr[half(s), :] = (proj + head_bias(layer, 2)).astype(BF16).astype(F32)
 
-        after_proj()
         for i in range(hb // 8):
             octet = s * (hb // 8) + i
             r8 = pl.ds(octet * 8, 8)
@@ -248,19 +244,19 @@
             exps = jnp.exp(scores - peak)
             w = (exps / jnp.sum(exps, axis=1, keepdims=True)).astype(BF16)
             if i == 0:
-                middle()
+                early()
+            if i == hb // 8 - 1:
+                late()
             cross_copy(layer, 1, octet).wait()
             o16 = lax.dot_general(w, vbuf[at, :], NT, preferred_element_type=F32)
             oscr[r8, :] = fold_heads(o16)
         return jnp.dot(oscr[half(s), :].astype(BF16), wout[layer, 1], preferred_element_type=F32)
 
-    def mlp_block(layer, s, after_proj, middle):
+    def mlp_block(layer, s, early, late):
         hidden = norm_rows(xres[half(s), :], ln_layers[layer, 2])
         pre = jnp.dot(hidden, fc1[layer], preferred_element_type=F32) + b_fc1[layer:layer + 1, :]
         active = (0.5 * pre * (1.0 + lax.erf(pre * (0.5 ** 0.5)))).astype(BF16)
-        out = jnp.dot(active, fc2[layer], preferred_element_type=F32)
-        middle()
-        return out
+        return jnp.dot(active, fc2[layer], preferred_element_type=F32)
 
     def write_new(layer, s):
         t = lax.broadcasted_iota(jnp.int32, (rows_per, ctx), 1)
@@ -316,12 +312,19 @@
         update(0)
         ready(layer, kind)
         share = functools.partial(sum_share, ph, 1)
-        sum_start(ph + 1, 0, block(layer, 0, share if kind < 2 else nothing, nothing))
-        if kind == 2:
+        gather = functools.partial(sum_chips, ph + 1, 0)
+        if kind == 1:
+            sum_start(ph + 1, 0, block(layer, 0, nothing, share))
+            pump(2)
+            update(1)
+            sum_start(ph + 1, 1, block(layer, 1, gather, nothing))
+        else:
+            sum_start(ph + 1, 0, block(layer, 0, nothing, nothing))
+            gather()
             share()
-        pump(2)
-        update(1)
-        sum_start(ph + 1, 1, block(layer, 1, nothing, functools.partial(sum_chips, ph + 1, 0)))
+            pump(2)
+            update(1)
+            sum_start(ph + 1, 1, block(layer, 1, nothing, nothing))
         if kind == 0:
             write_new(layer, 0)
         sum_chips(ph + 1, 1)

time: 79.4 us -> 76.8 us (0.967)
  Pallas kernels: 78.2 us -> 75.7 us
    pallas_call x1, Pallas kernels: 67.9 us -> 65.5 us  [local_step(): pl.pallas_call(functools.partial(decoder_kernel, (layers, batch, ctx, fra...]
where the time goes in v6:
time: 76.8 us; the launch traced here: 76.5 us
  Pallas kernels  75.7 us (99%)
  between operations  0.81 us (1%)
    pallas_call x1, Pallas kernels, local_step(): pl.pallas_call(functools.partial(decoder_kernel, (layers, batch, ctx, fra...  65.5 us
    pallas_call x1, Pallas kernels, local_step(): pl.pallas_call(final_kernel, out_shape=(jax.ShapeDtypeStruct((batch, voca...  6.69 us
    pallas_call x1, Pallas kernels, local_step(): pl.pallas_call(gather_kernel, out_shape=(pltpu.VMEM((batch, d), BF16), pl...  3.53 us

profile of v6, /device:TPU:0, one launch (start us, length us, event | category | flops | bytes accessed | tf_op | source)
XLA Modules:
  0.0 76.5 jit_solution(3406628069744609441)
XLA Ops:
  0.6 3.5 %gather_rows.1 = (bf16[32,1024]{1,0:T(8,128)(2,1)S(1)}, f32[32,1024]{1,0:T(8,128)S(1)}) custom-call(s32[32]{0:T(128)} %tok_ref.1, s32[32]{0:T(128)} %pos_smem.1, s32[1,32]{1,0:T(1,128)} %bitcast.37, s32[1,32]{1,0:T(1,128)} %bitcast.36, bf16[6528,1024]{1,0:T(8,128)(2,1)} %emb_hbm.3, bf16[448,1024]{1,0:T(8,128)(2,1)} %pos_hbm.1), custom_call_target="tpu_custom_call" | custom-call | tf_op jit(solution)/shard_map/gather_rows/pallas_call | solution.py:386
  4.2 65.5 %decoder_layers.1 = (bf16[2,2,4096,448]{3,2,1,0:T(8,128)(2,1)S(1)}, bf16[6528,1024]{1,0:T(8,128)(2,1)S(1)}, bf16[32,1024]{1,0:T(8,128)(2,1)S(1)}) custom-call(s32[32]{0:T(128)} %pos_smem.1, bf16[32,1024]{1,0:T(8,128)(2,1)S(1)} %get-tuple-element.11.picked_ref, f32[32,1024]{1,0:T(8,128)S(1)} %get-tuple-element.12.posrow_ref, f32[2,3,2,64]{3,2,1,0:T(2,128)} %in_bias_hbm.1, ...), custom_call_target="tpu_custom_call" | custom-call | tf_op jit(solution)/shard_map/decoder_layers/pallas_call | solution.py:396
  69.7 6.7 %final_logits.1 = (f32[32,6528]{1,0:T(8,128)}, bf16[2,4096,448]{2,1,0:T(8,128)(2,1)}, bf16[2,4096,448]{2,1,0:T(8,128)(2,1)}) custom-call(bf16[2,2,4096,448]{3,2,1,0:T(8,128)(2,1)S(1)} %get-tuple-element.13.kv_ref, bf16[6528,1024]{1,0:T(8,128)(2,1)S(1)} %get-tuple-element.14.e_ref, bf16[32,1024]{1,0:T(8,128)(2,1)S(1)} %get-tuple-element.15.fh_ref), custom_call_target="tpu_custom_call" | custom-call | tf_op jit(solution)/shard_map/final_logits/pallas_call | solution.py:424

commit v7 on v6

--- a/solution.py
+++ b/solution.py
@@ -233,23 +233,23 @@
         proj = lax.dot_general(hidden, wcq[layer], NT, preferred_element_type=F32)
         qscr[half(s), :] = (proj + head_bias(layer, 2)).astype(BF16).astype(F32)
 
-        for i in range(hb // 8):
-            octet = s * (hb // 8) + i
-            r8 = pl.ds(octet * 8, 8)
-            at = pl.ds(octet * 1024, 1024)
-            _, qbd = block_diag(qscr[r8, :])
+        octets = range(s * (hb // 8), (s + 1) * (hb // 8))
+        for octet in octets:
             cross_copy(layer, 0, octet).wait()
-            scores = jnp.dot(qbd, kbuf[at, :], preferred_element_type=F32) * 0.125
-            peak = jnp.max(scores, axis=1, keepdims=True)
-            exps = jnp.exp(scores - peak)
+        scores = []
+        for octet in octets:
+            _, qbd = block_diag(qscr[pl.ds(octet * 8, 8), :])
+            scores.append(jnp.dot(qbd, kbuf[pl.ds(octet * 1024, 1024), :], preferred_element_type=F32) * 0.125)
+        early()
+        for octet in octets:
+            cross_copy(layer, 1, octet).wait()
+        for octet, sc in zip(octets, scores):
+            exps = jnp.exp(sc - jnp.max(sc, axis=1, keepdims=True))
             w = (exps / jnp.sum(exps, axis=1, keepdims=True)).astype(BF16)
-            if i == 0:
-                early()
-            if i == hb // 8 - 1:
+            if octet == octets[-1]:
                 late()
-            cross_copy(layer, 1, octet).wait()
-            o16 = lax.dot_general(w, vbuf[at, :], NT, preferred_element_type=F32)
-            oscr[r8, :] = fold_heads(o16)
+            o16 = lax.dot_general(w, vbuf[pl.ds(octet * 1024, 1024), :], NT, preferred_element_type=F32)
+            oscr[pl.ds(octet * 8, 8), :] = fold_heads(o16)
         return jnp.dot(oscr[half(s), :].astype(BF16), wout[layer, 1], preferred_element_type=F32)
 
     def mlp_block(layer, s, early, late):
@@ -290,7 +290,8 @@
     pump(2)
     for c in small:
         c.wait()
-    sum_share(0, 0)
+    for s in range(2):
+        sum_share(0, s)
     for ph in range(3 * layers + 1):
         layer, kind = divmod(ph, 3)
         before, prev_kind = divmod(ph - 1, 3)
@@ -320,17 +321,20 @@
             sum_start(ph + 1, 1, block(layer, 1, gather, nothing))
         else:
             sum_start(ph + 1, 0, block(layer, 0, nothing, nothing))
-            gather()
-            share()
+            if kind == 2:
+                write_new(layer, 0)
+                gather()
+                write_new(layer, 1)
+                share()
+            else:
+                if ph > 0:
+                    share()
+                gather()
             pump(2)
             update(1)
             sum_start(ph + 1, 1, block(layer, 1, nothing, nothing))
-        if kind == 0:
-            write_new(layer, 0)
         sum_chips(ph + 1, 1)
         pump(2)
-        if kind == 0:
-            write_new(layer, 1)
         sum_share(ph + 1, 0)
     for i in range(4):
         e_copy(i).wait()

time: 76.8 us -> 76.4 us (level)
  no operation moved by 1% of the time
where the time goes in v7:
time: 76.4 us; the launch traced here: 76.1 us
  Pallas kernels  75.3 us (99%)
  between operations  0.81 us (1%)
    pallas_call x1, Pallas kernels, local_step(): pl.pallas_call(functools.partial(decoder_kernel, (layers, batch, ctx, fra...  65.1 us
    pallas_call x1, Pallas kernels, local_step(): pl.pallas_call(final_kernel, out_shape=(jax.ShapeDtypeStruct((batch, voca...  6.69 us
    pallas_call x1, Pallas kernels, local_step(): pl.pallas_call(gather_kernel, out_shape=(pltpu.VMEM((batch, d), BF16), pl...  3.47 us

profile of v7, /device:TPU:0, one launch (start us, length us, event | category | flops | bytes accessed | tf_op | source)
XLA Modules:
  0.0 76.1 jit_solution(1817797805767874335)
XLA Ops:
  0.6 3.5 %gather_rows.1 = (bf16[32,1024]{1,0:T(8,128)(2,1)S(1)}, f32[32,1024]{1,0:T(8,128)S(1)}) custom-call(s32[32]{0:T(128)} %tok_ref.1, s32[32]{0:T(128)} %pos_smem.1, s32[1,32]{1,0:T(1,128)} %bitcast.37, s32[1,32]{1,0:T(1,128)} %bitcast.36, bf16[6528,1024]{1,0:T(8,128)(2,1)} %emb_hbm.3, bf16[448,1024]{1,0:T(8,128)(2,1)} %pos_hbm.1), custom_call_target="tpu_custom_call" | custom-call | tf_op jit(solution)/shard_map/gather_rows/pallas_call | solution.py:390
  4.1 65.1 %decoder_layers.1 = (bf16[2,2,4096,448]{3,2,1,0:T(8,128)(2,1)S(1)}, bf16[6528,1024]{1,0:T(8,128)(2,1)S(1)}, bf16[32,1024]{1,0:T(8,128)(2,1)S(1)}) custom-call(s32[32]{0:T(128)} %pos_smem.1, bf16[32,1024]{1,0:T(8,128)(2,1)S(1)} %get-tuple-element.11.picked_ref, f32[32,1024]{1,0:T(8,128)S(1)} %get-tuple-element.12.posrow_ref, f32[2,3,2,64]{3,2,1,0:T(2,128)} %in_bias_hbm.1, ...), custom_call_target="tpu_custom_call" | custom-call | tf_op jit(solution)/shard_map/decoder_layers/pallas_call | solution.py:400
  69.2 6.7 %final_logits.1 = (f32[32,6528]{1,0:T(8,128)}, bf16[2,4096,448]{2,1,0:T(8,128)(2,1)}, bf16[2,4096,448]{2,1,0:T(8,128)(2,1)}) custom-call(bf16[2,2,4096,448]{3,2,1,0:T(8,128)(2,1)S(1)} %get-tuple-element.13.kv_ref, bf16[6528,1024]{1,0:T(8,128)(2,1)S(1)} %get-tuple-element.14.e_ref, bf16[32,1024]{1,0:T(8,128)(2,1)S(1)} %get-tuple-element.15.fh_ref), custom_call_target="tpu_custom_call" | custom-call | tf_op jit(solution)/shard_map/final_logits/pallas_call | solution.py:428

commit v8 on v7

--- a/solution.py
+++ b/solution.py
@@ -285,9 +285,9 @@
 
     for s in range(2):
         sum_start(0, s, picked_ref[half(s), :])
+    pump(9)
     for s in range(2):
         sum_chips(0, s)
-    pump(2)
     for c in small:
         c.wait()
     for s in range(2):
@@ -316,7 +316,6 @@
         gather = functools.partial(sum_chips, ph + 1, 0)
         if kind == 1:
             sum_start(ph + 1, 0, block(layer, 0, nothing, share))
-            pump(2)
             update(1)
             sum_start(ph + 1, 1, block(layer, 1, gather, nothing))
         else:
@@ -330,11 +329,15 @@
                 if ph > 0:
                     share()
                 gather()
-            pump(2)
+            if ph == 0:
+                pump(3)
+            if ph == 2:
+                pump(4)
             update(1)
             sum_start(ph + 1, 1, block(layer, 1, nothing, nothing))
         sum_chips(ph + 1, 1)
-        pump(2)
+        if ph == 1:
+            pump(9)
         sum_share(ph + 1, 0)
     for i in range(4):
         e_copy(i).wait()

time: 76.4 us -> 73.2 us (0.958)
  Pallas kernels: 75.3 us -> 72 us
    pallas_call x1, Pallas kernels: 65.1 us -> 61.8 us  [local_step(): pl.pallas_call(functools.partial(decoder_kernel, (layers, batch, ctx, fra...]
where the time goes in v8:
time: 73.2 us; the launch traced here: 72.8 us
  Pallas kernels  72 us (98%)
  between operations  0.81 us (1%)
    pallas_call x1, Pallas kernels, local_step(): pl.pallas_call(functools.partial(decoder_kernel, (layers, batch, ctx, fra...  61.8 us
    pallas_call x1, Pallas kernels, local_step(): pl.pallas_call(final_kernel, out_shape=(jax.ShapeDtypeStruct((batch, voca...  6.69 us
    pallas_call x1, Pallas kernels, local_step(): pl.pallas_call(gather_kernel, out_shape=(pltpu.VMEM((batch, d), BF16), pl...  3.51 us

profile of v8, /device:TPU:0, one launch (start us, length us, event | category | flops | bytes accessed | tf_op | source)
XLA Modules:
  0.0 72.8 jit_solution(16439163791861618419)
XLA Ops:
  0.6 3.5 %gather_rows.1 = (bf16[32,1024]{1,0:T(8,128)(2,1)S(1)}, f32[32,1024]{1,0:T(8,128)S(1)}) custom-call(s32[32]{0:T(128)} %tok_ref.1, s32[32]{0:T(128)} %pos_smem.1, s32[1,32]{1,0:T(1,128)} %bitcast.37, s32[1,32]{1,0:T(1,128)} %bitcast.36, bf16[6528,1024]{1,0:T(8,128)(2,1)} %emb_hbm.3, bf16[448,1024]{1,0:T(8,128)(2,1)} %pos_hbm.1), custom_call_target="tpu_custom_call" | custom-call | tf_op jit(solution)/shard_map/gather_rows/pallas_call | solution.py:393
  4.2 61.8 %decoder_layers.1 = (bf16[2,2,4096,448]{3,2,1,0:T(8,128)(2,1)S(1)}, bf16[6528,1024]{1,0:T(8,128)(2,1)S(1)}, bf16[32,1024]{1,0:T(8,128)(2,1)S(1)}) custom-call(s32[32]{0:T(128)} %pos_smem.1, bf16[32,1024]{1,0:T(8,128)(2,1)S(1)} %get-tuple-element.11.picked_ref, f32[32,1024]{1,0:T(8,128)S(1)} %get-tuple-element.12.posrow_ref, f32[2,3,2,64]{3,2,1,0:T(2,128)} %in_bias_hbm.1, ...), custom_call_target="tpu_custom_call" | custom-call | tf_op jit(solution)/shard_map/decoder_layers/pallas_call | solution.py:403
  66.0 6.7 %final_logits.1 = (f32[32,6528]{1,0:T(8,128)}, bf16[2,4096,448]{2,1,0:T(8,128)(2,1)}, bf16[2,4096,448]{2,1,0:T(8,128)(2,1)}) custom-call(bf16[2,2,4096,448]{3,2,1,0:T(8,128)(2,1)S(1)} %get-tuple-element.13.kv_ref, bf16[6528,1024]{1,0:T(8,128)(2,1)S(1)} %get-tuple-element.14.e_ref, bf16[32,1024]{1,0:T(8,128)(2,1)S(1)} %get-tuple-element.15.fh_ref), custom_call_target="tpu_custom_call" | custom-call | tf_op jit(solution)/shard_map/final_logits/pallas_call | solution.py:431

commit v9 on v8

--- a/solution.py
+++ b/solution.py
@@ -157,16 +157,20 @@
     def wait_for(ref, sem):
         pltpu.make_async_copy(ref, ref, sem).wait()
 
-    def sum_start(ph, s, value):
+    def columns(which):
+        return pl.ds(pl.multiple_of(which * wide, 128), wide)
+
+    def sum_start(ph, s, operands):
         mine, got, _, _ = bufs(ph, s)
-        mine[0] = value[:, :wide]
-        mine[1] = value[:, wide:]
-        send(mine.at[1 - core], got, ph, s, 0, partner)
+        lhs, weight = operands
+        mine[1] = jnp.dot(lhs, weight[:, columns(1 - core)], preferred_element_type=F32)
+        send(mine.at[1], got, ph, s, 0, partner)
+        mine[0] = jnp.dot(lhs, weight[:, columns(core)], preferred_element_type=F32)
 
     def sum_chips(ph, s):
         mine, got, by_chip, _ = bufs(ph, s)
         wait_for(got, recv_sem.at[ph, s, 0])
-        by_chip[chip] = mine[core] + got[...]
+        by_chip[chip] = mine[0] + got[...]
         for k in range(1, TP // 2):
             send(by_chip.at[chip], by_chip.at[chip], ph, s, 1, {'tp': 2 * lax.rem(chip + k, TP // 2) + core})
         wait_for(got, send_sem.at[ph, s, 0])
@@ -226,7 +230,7 @@
             o16 = lax.dot_general(past_w, vo[layer, at, :], NT, preferred_element_type=F32)
             lane = lax.broadcasted_iota(jnp.int32, (8, 128), 1)
             oscr[r8, :] = fold_heads(o16) + jnp.where(lane < 64, new_w[0:8], new_w[8:16]) * vn
-        return jnp.dot(oscr[half(s), :].astype(BF16), wout[layer, 0], preferred_element_type=F32)
+        return oscr[half(s), :].astype(BF16), wout.at[layer, 0]
 
     def cross_block(layer, s, early, late):
         hidden = norm_rows(xres[half(s), :], ln_layers[layer, 1])
@@ -245,18 +249,18 @@
             cross_copy(layer, 1, octet).wait()
         for octet, sc in zip(octets, scores):
             exps = jnp.exp(sc - jnp.max(sc, axis=1, keepdims=True))
-            w = (exps / jnp.sum(exps, axis=1, keepdims=True)).astype(BF16)
+            w = (exps * (1.0 / jnp.sum(exps, axis=1, keepdims=True))).astype(BF16)
             if octet == octets[-1]:
                 late()
             o16 = lax.dot_general(w, vbuf[pl.ds(octet * 1024, 1024), :], NT, preferred_element_type=F32)
             oscr[pl.ds(octet * 8, 8), :] = fold_heads(o16)
-        return jnp.dot(oscr[half(s), :].astype(BF16), wout[layer, 1], preferred_element_type=F32)
+        return oscr[half(s), :].astype(BF16), wout.at[layer, 1]
 
     def mlp_block(layer, s, early, late):
         hidden = norm_rows(xres[half(s), :], ln_layers[layer, 2])
         pre = jnp.dot(hidden, fc1[layer], preferred_element_type=F32) + b_fc1[layer:layer + 1, :]
         active = (0.5 * pre * (1.0 + lax.erf(pre * (0.5 ** 0.5)))).astype(BF16)
-        return jnp.dot(active, fc2[layer], preferred_element_type=F32)
+        return active, fc2.at[layer]
 
     def write_new(layer, s):
         t = lax.broadcasted_iota(jnp.int32, (rows_per, ctx), 1)
@@ -284,7 +288,10 @@
             w_copy(4, nl).wait()
 
     for s in range(2):
-        sum_start(0, s, picked_ref[half(s), :])
+        mine, got = stage0.at[s], pair0.at[s]
+        mine[0] = picked_ref[half(s), columns(core)]
+        mine[1] = picked_ref[half(s), columns(1 - core)]
+        send(mine.at[1], got, 0, s, 0, partner)
     pump(9)
     for s in range(2):
         sum_chips(0, s)
@@ -323,8 +330,8 @@
             if kind == 2:
                 write_new(layer, 0)
                 gather()
+                share()
                 write_new(layer, 1)
-                share()
             else:
                 if ph > 0:
                     share()

time: 73.2 us -> 72.9 us (level)
  no operation moved by 1% of the time
where the time goes in v9:
time: 72.9 us; the launch traced here: 72.6 us
  Pallas kernels  71.8 us (98%)
  between operations  0.81 us (1%)
    pallas_call x1, Pallas kernels, local_step(): pl.pallas_call(functools.partial(decoder_kernel, (layers, batch, ctx, fra...  61.7 us
    pallas_call x1, Pallas kernels, local_step(): pl.pallas_call(final_kernel, out_shape=(jax.ShapeDtypeStruct((batch, voca...  6.7 us
    pallas_call x1, Pallas kernels, local_step(): pl.pallas_call(gather_kernel, out_shape=(pltpu.VMEM((batch, d), BF16), pl...  3.45 us

profile of v9, /device:TPU:0, one launch (start us, length us, event | category | flops | bytes accessed | tf_op | source)
XLA Modules:
  0.0 72.6 jit_solution(7050851421251275396)
XLA Ops:
  0.6 3.4 %gather_rows.1 = (bf16[32,1024]{1,0:T(8,128)(2,1)S(1)}, f32[32,1024]{1,0:T(8,128)S(1)}) custom-call(s32[32]{0:T(128)} %tok_ref.1, s32[32]{0:T(128)} %pos_smem.1, s32[1,32]{1,0:T(1,128)} %bitcast.37, s32[1,32]{1,0:T(1,128)} %bitcast.36, bf16[6528,1024]{1,0:T(8,128)(2,1)} %emb_hbm.3, bf16[448,1024]{1,0:T(8,128)(2,1)} %pos_hbm.1), custom_call_target="tpu_custom_call" | custom-call | tf_op jit(solution)/shard_map/gather_rows/pallas_call | solution.py:400
  4.1 61.7 %decoder_layers.1 = (bf16[2,2,4096,448]{3,2,1,0:T(8,128)(2,1)S(1)}, bf16[6528,1024]{1,0:T(8,128)(2,1)S(1)}, bf16[32,1024]{1,0:T(8,128)(2,1)S(1)}) custom-call(s32[32]{0:T(128)} %pos_smem.1, bf16[32,1024]{1,0:T(8,128)(2,1)S(1)} %get-tuple-element.11.picked_ref, f32[32,1024]{1,0:T(8,128)S(1)} %get-tuple-element.12.posrow_ref, f32[2,3,2,64]{3,2,1,0:T(2,128)} %in_bias_hbm.1, ...), custom_call_target="tpu_custom_call" | custom-call | tf_op jit(solution)/shard_map/decoder_layers/pallas_call | solution.py:410
  65.8 6.7 %final_logits.1 = (f32[32,6528]{1,0:T(8,128)}, bf16[2,4096,448]{2,1,0:T(8,128)(2,1)}, bf16[2,4096,448]{2,1,0:T(8,128)(2,1)}) custom-call(bf16[2,2,4096,448]{3,2,1,0:T(8,128)(2,1)S(1)} %get-tuple-element.13.kv_ref, bf16[6528,1024]{1,0:T(8,128)(2,1)S(1)} %get-tuple-element.14.e_ref, bf16[32,1024]{1,0:T(8,128)(2,1)S(1)} %get-tuple-element.15.fh_ref), custom_call_target="tpu_custom_call" | custom-call | tf_op jit(solution)/shard_map/final_logits/pallas_call | solution.py:438

commit v10 on v9

--- a/solution.py
+++ b/solution.py
@@ -171,8 +171,8 @@
         mine, got, by_chip, _ = bufs(ph, s)
         wait_for(got, recv_sem.at[ph, s, 0])
         by_chip[chip] = mine[0] + got[...]
-        for k in range(1, TP // 2):
-            send(by_chip.at[chip], by_chip.at[chip], ph, s, 1, {'tp': 2 * lax.rem(chip + k, TP // 2) + core})
+        for other in (TP // 2 - 1 - chip, chip + 1 - 2 * lax.rem(chip, 2), lax.rem(chip + 2, TP // 2)):
+            send(by_chip.at[chip], by_chip.at[chip], ph, s, 1, {'tp': 2 * other + core})
         wait_for(got, send_sem.at[ph, s, 0])
 
     def sum_share(ph, s):
@@ -244,7 +244,8 @@
         for octet in octets:
             _, qbd = block_diag(qscr[pl.ds(octet * 8, 8), :])
             scores.append(jnp.dot(qbd, kbuf[pl.ds(octet * 1024, 1024), :], preferred_element_type=F32) * 0.125)
-        early()
+            if octet == octets[0]:
+                early()
         for octet in octets:
             cross_copy(layer, 1, octet).wait()
         for octet, sc in zip(octets, scores):

time: 72.9 us -> 71.5 us (0.981)
  Pallas kernels: 71.8 us -> 70.4 us
    pallas_call x1, Pallas kernels: 61.7 us -> 60.2 us  [local_step(): pl.pallas_call(functools.partial(decoder_kernel, (layers, batch, ctx, fra...]
where the time goes in v10:
time: 71.5 us; the launch traced here: 71.2 us
  Pallas kernels  70.4 us (98%)
  between operations  0.81 us (1%)
    pallas_call x1, Pallas kernels, local_step(): pl.pallas_call(functools.partial(decoder_kernel, (layers, batch, ctx, fra...  60.2 us
    pallas_call x1, Pallas kernels, local_step(): pl.pallas_call(final_kernel, out_shape=(jax.ShapeDtypeStruct((batch, voca...  6.69 us
    pallas_call x1, Pallas kernels, local_step(): pl.pallas_call(gather_kernel, out_shape=(pltpu.VMEM((batch, d), BF16), pl...  3.52 us

profile of v10, /device:TPU:0, one launch (start us, length us, event | category | flops | bytes accessed | tf_op | source)
XLA Modules:
  0.0 71.2 jit_solution(7516496441463355605)
XLA Ops:
  0.6 3.5 %gather_rows.1 = (bf16[32,1024]{1,0:T(8,128)(2,1)S(1)}, f32[32,1024]{1,0:T(8,128)S(1)}) custom-call(s32[32]{0:T(128)} %tok_ref.1, s32[32]{0:T(128)} %pos_smem.1, s32[1,32]{1,0:T(1,128)} %bitcast.37, s32[1,32]{1,0:T(1,128)} %bitcast.36, bf16[6528,1024]{1,0:T(8,128)(2,1)} %emb_hbm.3, bf16[448,1024]{1,0:T(8,128)(2,1)} %pos_hbm.1), custom_call_target="tpu_custom_call" | custom-call | tf_op jit(solution)/shard_map/gather_rows/pallas_call | solution.py:401
  4.2 60.2 %decoder_layers.1 = (bf16[2,2,4096,448]{3,2,1,0:T(8,128)(2,1)S(1)}, bf16[6528,1024]{1,0:T(8,128)(2,1)S(1)}, bf16[32,1024]{1,0:T(8,128)(2,1)S(1)}) custom-call(s32[32]{0:T(128)} %pos_smem.1, bf16[32,1024]{1,0:T(8,128)(2,1)S(1)} %get-tuple-element.11.picked_ref, f32[32,1024]{1,0:T(8,128)S(1)} %get-tuple-element.12.posrow_ref, f32[2,3,2,64]{3,2,1,0:T(2,128)} %in_bias_hbm.1, ...), custom_call_target="tpu_custom_call" | custom-call | tf_op jit(solution)/shard_map/decoder_layers/pallas_call | solution.py:411
  64.3 6.7 %final_logits.1 = (f32[32,6528]{1,0:T(8,128)}, bf16[2,4096,448]{2,1,0:T(8,128)(2,1)}, bf16[2,4096,448]{2,1,0:T(8,128)(2,1)}) custom-call(bf16[2,2,4096,448]{3,2,1,0:T(8,128)(2,1)S(1)} %get-tuple-element.13.kv_ref, bf16[6528,1024]{1,0:T(8,128)(2,1)S(1)} %get-tuple-element.14.e_ref, bf16[32,1024]{1,0:T(8,128)(2,1)S(1)} %get-tuple-element.15.fh_ref), custom_call_target="tpu_custom_call" | custom-call | tf_op jit(solution)/shard_map/final_logits/pallas_call | solution.py:439
